TPU v7x, 512 devices: a whole 4x8x8 slice. The times are simulated.
512 devices in a mesh: leaf: 128 (over z, y, core), sub: 4 (over x).
Axes of the slice: x: 4, y: 8, z: 8, core: 2. Of those that a mesh axis runs over, the one named last changes fastest.
Arguments:
- signal: bfloat16 [32, 1048576], P(None, ('leaf', 'sub')), may hold values from -6 to 6
- row_basis: bfloat16 [64, 1048576], P(None, ('leaf', 'sub')), may hold values from -0.375 to 0.375
- transfer: bfloat16 [8192, 13, 32, 128], P(('leaf', 'sub')), may hold values from -0.5 to 0.5
- column_basis: bfloat16 [64, 1048576], P(None, ('leaf', 'sub')), may hold values from -0.75 to 0.75
- near_blocks: bfloat16 [12288, 128, 256], P(('leaf', 'sub')), may hold values from -0.375 to 0.375
- near_list: int32 [12288, 2], P(('leaf', 'sub')), may hold values from -1 to 31, as said below
Outputs:
- result: float32 [32, 1048576], P(None, ('leaf', 'sub'))
Inputs may be any that keep to these rules, and one draw needn't show every extreme that they name: `near_list`: on each device the live entries (column >= 0) fill a leading run of its 24 slots, 2 or more of them, and empty slots hold -1 in both places; a live entry has 0 <= column < 24 and column <= row <= column + 8. Devices 2m and 2m + 1 hold at most 24 live entries together, and some such pair holds 24.
All inputs are finite; a program needn't handle non-finite values.
Results may differ from a plain program's by a relative error of at most 0.0003.
Values may be sent and summed in bfloat16 or wider, within the bound.
A program may use at most 128 MiB of HBM per device.

v0:
```python
import jax
import jax.numpy as jnp
from jax import lax
from jax.sharding import PartitionSpec as P

LEAF = 128


highest = lax.Precision.HIGHEST


def with_halo(cells, sides, width):
    for axis, dim in sides:
        count = lax.axis_size(axis)
        head = lax.slice_in_dim(cells, 0, width, axis=dim)
        tail = lax.slice_in_dim(cells, cells.shape[dim] - width, cells.shape[dim], axis=dim)
        cells = jnp.concatenate(
            [
                lax.ppermute(tail, axis, [(i, (i + 1) % count) for i in range(count)]),
                cells,
                lax.ppermute(head, axis, [((i + 1) % count, i) for i in range(count)]),
            ],
            axis=dim,
        )
    return cells


def swapped(shard, axis, distance):
    return lax.ppermute(shard, axis, [(i, i ^ 1 << distance) for i in range(lax.axis_size(axis))])


def from_behind(value, axis, steps):
    count = lax.axis_size(axis)
    pairs = [(source, (source + steps) % count) for source in range(count)]
    return lax.ppermute(value, axis, pairs)


def project(signal, row_basis):
    rhs_count = signal.shape[0] // 2
    rank_width = row_basis.shape[0] // 2
    leaves = signal.shape[1] // LEAF
    samples = signal.reshape(2, rhs_count, leaves, LEAF)
    basis_rows = row_basis.reshape(2, rank_width, leaves, LEAF)
    products = jnp.einsum(
        "xrlp,yqlp->xylrq", samples, basis_rows, preferred_element_type=jnp.float32
    )
    real_part = products[0, 0] + products[1, 1]
    imag_part = products[1, 0] - products[0, 1]
    return jnp.transpose(jnp.concatenate([real_part, imag_part], axis=-1), (1, 0, 2))


def block_form(weights):
    matrices = weights.astype(jnp.float32)
    rank_width = matrices.shape[1]
    pieces = []
    for offspring in range(2):
        real_part = matrices[:, :, 2 * offspring * rank_width : (2 * offspring + 1) * rank_width]
        imag_part = matrices[
            :, :, (2 * offspring + 1) * rank_width : (2 * offspring + 2) * rank_width
        ]
        upper_rows = jnp.concatenate([real_part, -imag_part], axis=2)
        lower_rows = jnp.concatenate([imag_part, real_part], axis=2)
        pieces.append(jnp.concatenate([upper_rows, lower_rows], axis=1))
    return jnp.concatenate(pieces, axis=1)


def apply_level(paired, weights):
    return jnp.einsum("rsm,smn->rsn", paired, block_form(weights), precision=highest)


def pair_local(coeffs, height):
    rhs_count, slot_count, doubled = coeffs.shape
    half_span = 2 ** (height - 1)
    grouped = coeffs.reshape(rhs_count, slot_count // (2 * half_span), 2, half_span, doubled)
    joined = jnp.concatenate([grouped[:, :, 0], grouped[:, :, 1]], axis=-1)
    twice = jnp.stack([joined, joined], axis=2)
    return twice.reshape(rhs_count, slot_count, 2 * doubled)


def swap_level(owned, partner_box, upper_bit, weights):
    low_side = jnp.where(upper_bit == 0, owned, partner_box)
    high_side = jnp.where(upper_bit == 0, partner_box, owned)
    return apply_level(jnp.concatenate([low_side, high_side], axis=-1), weights)


def evaluate(coeffs, column_basis):
    rhs_count, leaves, doubled = coeffs.shape
    rank_width = doubled // 2
    basis_rows = column_basis.astype(jnp.float32).reshape(2, rank_width, leaves, LEAF)
    real_coefficient = coeffs[:, :, :rank_width]
    imag_coef = coeffs[:, :, rank_width:]
    real_out = jnp.einsum(
        "rlq,qlp->rlp", real_coefficient, basis_rows[0], precision=highest
    ) - jnp.einsum("rlq,qlp->rlp", imag_coef, basis_rows[1], precision=highest)
    imag_out = jnp.einsum("rlq,qlp->rlp", imag_coef, basis_rows[0], precision=highest) + jnp.einsum(
        "rlq,qlp->rlp", real_coefficient, basis_rows[1], precision=highest
    )
    return jnp.concatenate([real_out, imag_out], axis=0).reshape(2 * rhs_count, leaves * LEAF)


def near_products(picked, blocks):
    products = jnp.einsum("scp,spj->scj", picked, blocks, preferred_element_type=jnp.float32)
    rhs_count = picked.shape[1] // 2
    real_part = products[:, :rhs_count, :LEAF] + products[:, rhs_count:, LEAF:]
    imag_part = products[:, rhs_count:, :LEAF] - products[:, :rhs_count, LEAF:]
    return jnp.concatenate([real_part, imag_part], axis=1)


def accumulate(output_values, col_index, box_count):
    selector = (col_index[:, None] == jnp.arange(box_count, dtype=jnp.int32)[None, :]).astype(
        jnp.float32
    )
    return jnp.einsum("sw,scj->cwj", selector, output_values, precision=highest)


def shards(signal, row_basis, transfer, column_basis, near_blocks, near_list):
    channels = signal.shape[0]
    box_count = signal.shape[1] // LEAF
    reach_boxes = box_count // 4
    local_levels = box_count.bit_length() - 1
    sub_bits = lax.axis_size("sub").bit_length() - 1
    count_of_leaves = lax.axis_size("leaf")
    leaf_bits = count_of_leaves.bit_length() - 1
    sub_index = lax.axis_index("sub")
    leaf_index = lax.axis_index("leaf")
    window = with_halo(signal, ((("leaf", "sub"), 1),), 2 * reach_boxes * LEAF)
    coeffs = project(signal, row_basis)
    for height in range(1, local_levels + 1):
        coeffs = apply_level(pair_local(coeffs, height), transfer[:, height - 1])
    for bit_place in range(sub_bits):
        partner_box = swapped(coeffs, "sub", bit_place)
        coeffs = swap_level(
            coeffs, partner_box, sub_index >> bit_place & 1, transfer[:, local_levels + bit_place]
        )
    for bit_place in range(leaf_bits):
        partner_box = swapped(coeffs, "leaf", bit_place)
        coeffs = swap_level(
            coeffs,
            partner_box,
            leaf_index >> bit_place & 1,
            transfer[:, local_levels + sub_bits + bit_place],
        )
    far_field = evaluate(coeffs, column_basis)
    leaf_tiles = window.reshape(channels, -1, LEAF)
    row_index = near_list[:, 0]
    col_index = near_list[:, 1]
    picked = jnp.transpose(jnp.take(leaf_tiles, jnp.maximum(row_index, 0), axis=1), (1, 0, 2))
    out_boxes = box_count + 2 * reach_boxes
    near_field = accumulate(near_products(picked, near_blocks), col_index, out_boxes)
    from_next = from_behind(near_field[:, :reach_boxes], ("leaf", "sub"), -1)
    from_prev = from_behind(near_field[:, box_count + reach_boxes :], ("leaf", "sub"), 1)
    center = near_field[:, reach_boxes : reach_boxes + box_count]
    center = center.at[:, :reach_boxes].add(from_prev)
    center = center.at[:, box_count - reach_boxes :].add(from_next)
    return far_field + center.reshape(channels, box_count * LEAF)


def solution(mesh):
    return jax.shard_map(
        shards,
        mesh=mesh,
        in_specs=(
            P(None, ("leaf", "sub")),
            P(None, ("leaf", "sub")),
            P(("leaf", "sub"), None, None, None),
            P(None, ("leaf", "sub")),
            P(("leaf", "sub"), None, None),
            P(("leaf", "sub"), None),
        ),
        out_specs=P(None, ("leaf", "sub")),
        check_vma=False,
    )
```

profile of v0, /device:TPU:56, one launch (start us, length us, event | category | flops | bytes accessed | tf_op | source)
XLA Modules:
  0.0 139.6 jit_solution(15067877604897750269)
XLA Ops:
  0.0 1.1 copy.121
  1.2 0.9 copy.122
  2.7 1.1 fusion.273
  3.8 1.2 copy.111
  5.5 1.3 fusion.184
  7.6 1.3 fusion.168
  9.6 1.3 fusion.152
  11.6 1.9 %convolution_bitcast_fusion.10 = f32[16,16,64]{2,0,1:T(8,128)} fusion(f32[16,16,128]{2,0,1:T(8,128)S(1)} %bitcast.188, f32[16,32,32]{1,2,0:T(8,128)S(1)} %get-tuple-element.45, f32[16,32,32]{1,2,0:T(8,128)S(1)} %get-tuple-element.44, f32[16,32,32]{1,2,0:T(8,128)S(1)} %get-tuple-element.43, f32[16,32,32]{1,2,0:T(8,128)S(1)} %get-tuple-element.47, ...), kind=kOutput, calls=%fused_computation.11 | convolution fusion | flops 26083328 | bytes 589824 | tf_op jit(solution)/shard_map/rsm,smn->rsn/dot_general | solution.py:68
  13.5 3.4 %collective-permute-start = (f32[16,16,64]{2,0,1:T(8,128)}, f32[16,16,64]{2,0,1:T(8,128)}, u32[]{:S(2)}, u32[]{:S(2)}) collective-permute-start(f32[16,16,64]{2,0,1:T(8,128)} %convolution_bitcast_fusion.10), channel_id=1, source_target_pairs={{0,1},{1,0},{2,3},{3,2},{4,5},{5,4},{6,7},{7,6},{8,9},{9,8},{10,11... | collective-permute-start | bytes 196616 | tf_op jit(solution)/shard_map/ppermute | solution.py:29
  17.6 3.9 %collective-permute-start.10 = (bf16[32,1024]{1,0:T(8,128)(2,1)}, bf16[32,1024]{1,0:T(8,128)(2,1)}, u32[]{:S(2)}, u32[]{:S(2)}) collective-permute-start(bf16[32,1024]{1,0:T(8,128)(2,1)} %get-tuple-element.153), channel_id=1, source_target_pairs={{1,0},{2,1},{3,2},{4,3},{5,4},{6,5},{7,6},{8,7},{9,8},{10,9},{11,1... | collective-permute-start | bytes 196616 | tf_op jit(solution)/shard_map/ppermute | solution.py:21
  21.5 1.9 %collective-permute-start.9 = (bf16[32,1024]{1,0:T(8,128)(2,1)}, bf16[32,1024]{1,0:T(8,128)(2,1)}, u32[]{:S(2)}, u32[]{:S(2)}) collective-permute-start(bf16[32,1024]{1,0:T(8,128)(2,1)} %get-tuple-element.152), channel_id=1, source_target_pairs={{0,1},{1,2},{2,3},{3,4},{4,5},{5,6},{6,7},{7,8},{8,9},{9,10},{10,1... | collective-permute-start | bytes 196616 | tf_op jit(solution)/shard_map/ppermute | solution.py:19
  23.9 1.3 slice_negate_fusion.9
  25.6 1.3 slice_negate_fusion.11
  27.2 1.2 slice_negate_fusion.13
  28.8 1.3 slice_negate_fusion.15
  30.5 1.2 slice_negate_fusion.17
  32.2 1.3 slice_negate_fusion.19
  33.8 1.2 slice_negate_fusion.21
  35.4 1.2 slice_negate_fusion.23
  37.1 1.0 slice_negate_fusion.25
  38.2 1.0 broadcast_select_fusion.1
  39.2 1.3 convolution_bitcast_fusion.9
  40.5 4.8 %collective-permute-start.1 = (f32[16,16,64]{2,0,1:T(8,128)S(1)}, f32[16,16,64]{2,0,1:T(8,128)}, u32[]{:S(2)}, u32[]{:S(2)}) collective-permute-start(f32[16,16,64]{2,0,1:T(8,128)S(1)} %convolution_bitcast_fusion.9), channel_id=1, source_target_pairs={{0,2},{1,3},{2,0},{3,1},{4,6},{5,7},{6,4},{7,5},{8,10},{9,11},{10,... | collective-permute-start | bytes 196616 | tf_op jit(solution)/shard_map/ppermute | solution.py:29
  45.4 0.9 copy_bitcast_fusion.2
  46.9 2.7 %collective-permute-done.1 = f32[16,16,64]{2,0,1:T(8,128)} collective-permute-done((f32[16,16,64]{2,0,1:T(8,128)S(1)}, f32[16,16,64]{2,0,1:T(8,128)}, u32[]{:S(2)}, u32[]{:S(2)}) %collective-permute-start.1) | collective-permute-done | bytes 65568 | tf_op jit(solution)/shard_map/ppermute | solution.py:29
  49.6 0.9 broadcast_select_fusion.3
  50.5 2.8 %convolution_bitcast_fusion.8 = f32[16,16,64]{2,0,1:T(8,128)S(1)} fusion(f32[16,32,32]{1,2,0:T(8,128)} %get-tuple-element.75, f32[16,32,32]{1,2,0:T(8,128)} %get-tuple-element.74, f32[16,32,32]{1,2,0:T(8,128)} %get-tuple-element.73, f32[16,32,32]{1,2,0:T(8,128)} %get-tuple-element.77, f32[16,32,32]{1,2,0:T(8,128)} %get-tuple-element.76, ...), kind=kOutput, calls=%fused_computation.9 | convolution fusion | flops 26116096 | bytes 589824 | tf_op jit(solution)/shard_map/rsm,smn->rsn/dot_general | solution.py:68
  53.4 2.1 %collective-permute-start.2 = (f32[16,16,64]{2,0,1:T(8,128)S(1)}, f32[16,16,64]{2,0,1:T(8,128)S(1)}, u32[]{:S(2)}, u32[]{:S(2)}) collective-permute-start(f32[16,16,64]{2,0,1:T(8,128)S(1)} %convolution_bitcast_fusion.8), channel_id=1, source_target_pairs={{0,4},{4,0},{8,12},{12,8},{16,20},{20,16},{24,28},{28,24},{32,36},... | collective-permute-start | bytes 196616 | tf_op jit(solution)/shard_map/ppermute | solution.py:29
  56.9 1.3 convolution_bitcast_fusion.7
  58.2 3.3 %collective-permute-start.3 = (f32[16,16,64]{2,0,1:T(8,128)S(1)}, f32[16,16,64]{2,0,1:T(8,128)S(1)}, u32[]{:S(2)}, u32[]{:S(2)}) collective-permute-start(f32[16,16,64]{2,0,1:T(8,128)S(1)} %convolution_bitcast_fusion.7), channel_id=1, source_target_pairs={{0,8},{4,12},{8,0},{12,4},{16,24},{20,28},{24,16},{28,20},{32,40},... | collective-permute-start | bytes 196616 | tf_op jit(solution)/shard_map/ppermute | solution.py:29
  61.6 4.1 %collective-permute-done.3 = f32[16,16,64]{2,0,1:T(8,128)S(1)} collective-permute-done((f32[16,16,64]{2,0,1:T(8,128)S(1)}, f32[16,16,64]{2,0,1:T(8,128)S(1)}, u32[]{:S(2)}, u32[]{:S(2)}) %collective-permute-start.3) | collective-permute-done | bytes 65568 | tf_op jit(solution)/shard_map/ppermute | solution.py:29
  65.8 1.3 convolution_bitcast_fusion.6
  67.1 4.0 %collective-permute-start.4 = (f32[16,16,64]{2,0,1:T(8,128)S(1)}, f32[16,16,64]{2,0,1:T(8,128)S(1)}, u32[]{:S(2)}, u32[]{:S(2)}) collective-permute-start(f32[16,16,64]{2,0,1:T(8,128)S(1)} %convolution_bitcast_fusion.6), channel_id=1, source_target_pairs={{0,16},{4,20},{8,24},{12,28},{16,0},{20,4},{24,8},{28,12},{32,48},... | collective-permute-start | bytes 196616 | tf_op jit(solution)/shard_map/ppermute | solution.py:29
  71.2 6.2 %collective-permute-done.4 = f32[16,16,64]{2,0,1:T(8,128)S(1)} collective-permute-done((f32[16,16,64]{2,0,1:T(8,128)S(1)}, f32[16,16,64]{2,0,1:T(8,128)S(1)}, u32[]{:S(2)}, u32[]{:S(2)}) %collective-permute-start.4) | collective-permute-done | bytes 65568 | tf_op jit(solution)/shard_map/ppermute | solution.py:29
  77.5 1.3 convolution_bitcast_fusion.5
  78.9 11.5 %collective-permute-start.5 = (f32[16,16,64]{2,0,1:T(8,128)S(1)}, f32[16,16,64]{2,0,1:T(8,128)S(1)}, u32[]{:S(2)}, u32[]{:S(2)}) collective-permute-start(f32[16,16,64]{2,0,1:T(8,128)S(1)} %convolution_bitcast_fusion.5), channel_id=1, source_target_pairs={{0,32},{4,36},{8,40},{12,44},{16,48},{20,52},{24,56},{28,60},{32,0... | collective-permute-start | bytes 196616 | tf_op jit(solution)/shard_map/ppermute | solution.py:29
  91.0 3.7 %collective-permute-done.5 = f32[16,16,64]{2,0,1:T(8,128)S(1)} collective-permute-done((f32[16,16,64]{2,0,1:T(8,128)S(1)}, f32[16,16,64]{2,0,1:T(8,128)S(1)}, u32[]{:S(2)}, u32[]{:S(2)}) %collective-permute-start.5) | collective-permute-done | bytes 65568 | tf_op jit(solution)/shard_map/ppermute | solution.py:29
  94.9 1.3 convolution_bitcast_fusion.4
  96.2 1.9 %collective-permute-start.6 = (f32[16,16,64]{2,0,1:T(8,128)S(1)}, f32[16,16,64]{2,0,1:T(8,128)S(1)}, u32[]{:S(2)}, u32[]{:S(2)}) collective-permute-start(f32[16,16,64]{2,0,1:T(8,128)S(1)} %convolution_bitcast_fusion.4), channel_id=1, source_target_pairs={{0,64},{4,68},{8,72},{12,76},{16,80},{20,84},{24,88},{28,92},{32,9... | collective-permute-start | bytes 196616 | tf_op jit(solution)/shard_map/ppermute | solution.py:29
  98.2 2.8 %collective-permute-start.11 = (f32[32,4,128]{2,0,1:T(8,128)S(1)}, f32[32,4,128]{2,0,1:T(8,128)S(1)}, u32[]{:S(2)}, u32[]{:S(2)}) collective-permute-start(f32[32,4,128]{2,0,1:T(8,128)S(1)} %get-tuple-element.123), channel_id=1, source_target_pairs={{0,1},{1,2},{2,3},{3,4},{4,5},{5,6},{6,7},{7,8},{8,9},{9,10},{10,1... | collective-permute-start | bytes 196616 | tf_op jit(solution)/shard_map/ppermute | solution.py:35
  101.0 5.0 %collective-permute-start.12 = (f32[32,4,128]{2,0,1:T(8,128)S(1)}, f32[32,4,128]{2,0,1:T(8,128)S(1)}, u32[]{:S(2)}, u32[]{:S(2)}) collective-permute-start(f32[32,4,128]{2,0,1:T(8,128)S(1)} %get-tuple-element.122), channel_id=1, source_target_pairs={{0,511},{1,0},{2,1},{3,2},{4,3},{5,4},{6,5},{7,6},{8,7},{9,8},{10,... | collective-permute-start | bytes 196616 | tf_op jit(solution)/shard_map/ppermute | solution.py:35
  106.1 1.3 convolution_bitcast_fusion.3
  107.4 5.9 %collective-permute-start.7 = (f32[16,16,64]{2,0,1:T(8,128)S(1)}, f32[16,16,64]{2,0,1:T(8,128)S(1)}, u32[]{:S(2)}, u32[]{:S(2)}) collective-permute-start(f32[16,16,64]{2,0,1:T(8,128)S(1)} %convolution_bitcast_fusion.3), channel_id=1, source_target_pairs={{0,128},{4,132},{8,136},{12,140},{16,144},{20,148},{24,152},{28,15... | collective-permute-start | bytes 196616 | tf_op jit(solution)/shard_map/ppermute | solution.py:29
  113.4 6.6 %collective-permute-done.7 = f32[16,16,64]{2,0,1:T(8,128)S(1)} collective-permute-done((f32[16,16,64]{2,0,1:T(8,128)S(1)}, f32[16,16,64]{2,0,1:T(8,128)S(1)}, u32[]{:S(2)}, u32[]{:S(2)}) %collective-permute-start.7) | collective-permute-done | bytes 65568 | tf_op jit(solution)/shard_map/ppermute | solution.py:29
  120.0 1.3 convolution_bitcast_fusion.2
  121.3 8.6 %collective-permute-start.8 = (f32[16,16,64]{2,0,1:T(8,128)S(1)}, f32[16,16,64]{2,0,1:T(8,128)S(1)}, u32[]{:S(2)}, u32[]{:S(2)}) collective-permute-start(f32[16,16,64]{2,0,1:T(8,128)S(1)} %convolution_bitcast_fusion.2), channel_id=1, source_target_pairs={{0,256},{4,260},{8,264},{12,268},{16,272},{20,276},{24,280},{28,28... | collective-permute-start | bytes 196616 | tf_op jit(solution)/shard_map/ppermute | solution.py:29
  130.0 6.4 %collective-permute-done.8 = f32[16,16,64]{2,0,1:T(8,128)S(1)} collective-permute-done((f32[16,16,64]{2,0,1:T(8,128)S(1)}, f32[16,16,64]{2,0,1:T(8,128)S(1)}, u32[]{:S(2)}, u32[]{:S(2)}) %collective-permute-start.8) | collective-permute-done | bytes 65568 | tf_op jit(solution)/shard_map/ppermute | solution.py:29
  136.5 1.3 convolution_bitcast_fusion.1
  (188 shorter events, 12.1 us)
Async XLA Ops:
  0.0 55.5 %copy-start = (bf16[24,128,256]{2,1,0:T(8,128)(2,1)S(1)}, bf16[24,128,256]{2,1,0:T(8,128)(2,1)}, u32[]{:S(2)}) copy-start(bf16[24,128,256]{2,1,0:T(8,128)(2,1)} %param.14) | copy-start | bytes 4718596
  11.6 5.4 %copy-start.2 = (bf16[32,2048]{1,0:T(8,128)(2,1)S(1)}, bf16[32,2048]{1,0:T(8,128)(2,1)}, u32[]{:S(2)}) copy-start(bf16[32,2048]{1,0:T(8,128)(2,1)} %param.10) | copy-start | bytes 393220
  11.6 11.9 %copy-start.51 = (s32[24,2]{0,1:T(2,128)S(1)}, s32[24,2]{0,1:T(2,128)}, u32[]{:S(2)}) copy-start(s32[24,2]{0,1:T(2,128)} %param.15) | copy-start | bytes 580
  13.5 24.6 %collective-permute-start = (f32[16,16,64]{2,0,1:T(8,128)}, f32[16,16,64]{2,0,1:T(8,128)}, u32[]{:S(2)}, u32[]{:S(2)}) collective-permute-start(f32[16,16,64]{2,0,1:T(8,128)} %convolution_bitcast_fusion.10), channel_id=1, source_target_pairs={{0,1},{1,0},{2,3},{3,2},{4,5},{5,4},{6,7},{7,6},{8,9},{9,8},{10,11... | collective-permute-start | bytes 196616 | tf_op jit(solution)/shard_map/ppermute | solution.py:29
  17.6 27.7 %collective-permute-start.10 = (bf16[32,1024]{1,0:T(8,128)(2,1)}, bf16[32,1024]{1,0:T(8,128)(2,1)}, u32[]{:S(2)}, u32[]{:S(2)}) collective-permute-start(bf16[32,1024]{1,0:T(8,128)(2,1)} %get-tuple-element.153), channel_id=1, source_target_pairs={{1,0},{2,1},{3,2},{4,3},{5,4},{6,5},{7,6},{8,7},{9,8},{10,9},{11,1... | collective-permute-start | bytes 196616 | tf_op jit(solution)/shard_map/ppermute | solution.py:21
  21.5 23.8 %collective-permute-start.9 = (bf16[32,1024]{1,0:T(8,128)(2,1)}, bf16[32,1024]{1,0:T(8,128)(2,1)}, u32[]{:S(2)}, u32[]{:S(2)}) collective-permute-start(bf16[32,1024]{1,0:T(8,128)(2,1)} %get-tuple-element.152), channel_id=1, source_target_pairs={{0,1},{1,2},{2,3},{3,4},{4,5},{5,6},{6,7},{7,8},{8,9},{9,10},{10,1... | collective-permute-start | bytes 196616 | tf_op jit(solution)/shard_map/ppermute | solution.py:19
  40.5 9.1 %collective-permute-start.1 = (f32[16,16,64]{2,0,1:T(8,128)S(1)}, f32[16,16,64]{2,0,1:T(8,128)}, u32[]{:S(2)}, u32[]{:S(2)}) collective-permute-start(f32[16,16,64]{2,0,1:T(8,128)S(1)} %convolution_bitcast_fusion.9), channel_id=1, source_target_pairs={{0,2},{1,3},{2,0},{3,1},{4,6},{5,7},{6,4},{7,5},{8,10},{9,11},{10,... | collective-permute-start | bytes 196616 | tf_op jit(solution)/shard_map/ppermute | solution.py:29
  53.4 3.4 %collective-permute-start.2 = (f32[16,16,64]{2,0,1:T(8,128)S(1)}, f32[16,16,64]{2,0,1:T(8,128)S(1)}, u32[]{:S(2)}, u32[]{:S(2)}) collective-permute-start(f32[16,16,64]{2,0,1:T(8,128)S(1)} %convolution_bitcast_fusion.8), channel_id=1, source_target_pairs={{0,4},{4,0},{8,12},{12,8},{16,20},{20,16},{24,28},{28,24},{32,36},... | collective-permute-start | bytes 196616 | tf_op jit(solution)/shard_map/ppermute | solution.py:29
  56.9 8.8 %copy-start.32 = (f32[16,32,32]{1,2,0:T(8,128)S(1)}, f32[16,32,32]{1,2,0:T(8,128)}, u32[]{:S(2)}) copy-start(f32[16,32,32]{1,2,0:T(8,128)} %get-tuple-element.84) | copy-start | bytes 196612
  56.9 8.8 %copy-start.33 = (f32[16,32,32]{1,2,0:T(8,128)S(1)}, f32[16,32,32]{1,2,0:T(8,128)}, u32[]{:S(2)}) copy-start(f32[16,32,32]{1,2,0:T(8,128)} %get-tuple-element.85) | copy-start | bytes 196612
  56.9 8.8 %copy-start.34 = (f32[16,32,32]{1,2,0:T(8,128)S(1)}, f32[16,32,32]{1,2,0:T(8,128)}, u32[]{:S(2)}) copy-start(f32[16,32,32]{1,2,0:T(8,128)} %get-tuple-element.86) | copy-start | bytes 196612
  56.9 8.8 %copy-start.35 = (f32[16,32,32]{1,2,0:T(8,128)S(1)}, f32[16,32,32]{1,2,0:T(8,128)}, u32[]{:S(2)}) copy-start(f32[16,32,32]{1,2,0:T(8,128)} %get-tuple-element.87) | copy-start | bytes 196612
  56.9 8.8 %copy-start.36 = (f32[16,32,32]{1,2,0:T(8,128)S(1)}, f32[16,32,32]{1,2,0:T(8,128)}, u32[]{:S(2)}) copy-start(f32[16,32,32]{1,2,0:T(8,128)} %get-tuple-element.88) | copy-start | bytes 196612
  56.9 8.8 %copy-start.37 = (f32[16,32,32]{1,2,0:T(8,128)S(1)}, f32[16,32,32]{1,2,0:T(8,128)}, u32[]{:S(2)}) copy-start(f32[16,32,32]{1,2,0:T(8,128)} %get-tuple-element.89) | copy-start | bytes 196612
  58.2 7.4 %collective-permute-start.3 = (f32[16,16,64]{2,0,1:T(8,128)S(1)}, f32[16,16,64]{2,0,1:T(8,128)S(1)}, u32[]{:S(2)}, u32[]{:S(2)}) collective-permute-start(f32[16,16,64]{2,0,1:T(8,128)S(1)} %convolution_bitcast_fusion.7), channel_id=1, source_target_pairs={{0,8},{4,12},{8,0},{12,4},{16,24},{20,28},{24,16},{28,20},{32,40},... | collective-permute-start | bytes 196616 | tf_op jit(solution)/shard_map/ppermute | solution.py:29
  65.8 11.7 %copy-start.26 = (f32[16,32,32]{1,2,0:T(8,128)S(1)}, f32[16,32,32]{1,2,0:T(8,128)}, u32[]{:S(2)}) copy-start(f32[16,32,32]{1,2,0:T(8,128)} %get-tuple-element.90) | copy-start | bytes 196612
  65.8 11.7 %copy-start.27 = (f32[16,32,32]{1,2,0:T(8,128)S(1)}, f32[16,32,32]{1,2,0:T(8,128)}, u32[]{:S(2)}) copy-start(f32[16,32,32]{1,2,0:T(8,128)} %get-tuple-element.91) | copy-start | bytes 196612
  65.8 11.7 %copy-start.28 = (f32[16,32,32]{1,2,0:T(8,128)S(1)}, f32[16,32,32]{1,2,0:T(8,128)}, u32[]{:S(2)}) copy-start(f32[16,32,32]{1,2,0:T(8,128)} %get-tuple-element.92) | copy-start | bytes 196612
  65.8 11.7 %copy-start.29 = (f32[16,32,32]{1,2,0:T(8,128)S(1)}, f32[16,32,32]{1,2,0:T(8,128)}, u32[]{:S(2)}) copy-start(f32[16,32,32]{1,2,0:T(8,128)} %get-tuple-element.93) | copy-start | bytes 196612
  65.8 11.7 %copy-start.30 = (f32[16,32,32]{1,2,0:T(8,128)S(1)}, f32[16,32,32]{1,2,0:T(8,128)}, u32[]{:S(2)}) copy-start(f32[16,32,32]{1,2,0:T(8,128)} %get-tuple-element.94) | copy-start | bytes 196612
  65.8 11.7 %copy-start.31 = (f32[16,32,32]{1,2,0:T(8,128)S(1)}, f32[16,32,32]{1,2,0:T(8,128)}, u32[]{:S(2)}) copy-start(f32[16,32,32]{1,2,0:T(8,128)} %get-tuple-element.95) | copy-start | bytes 196612
  67.1 10.3 %collective-permute-start.4 = (f32[16,16,64]{2,0,1:T(8,128)S(1)}, f32[16,16,64]{2,0,1:T(8,128)S(1)}, u32[]{:S(2)}, u32[]{:S(2)}) collective-permute-start(f32[16,16,64]{2,0,1:T(8,128)S(1)} %convolution_bitcast_fusion.6), channel_id=1, source_target_pairs={{0,16},{4,20},{8,24},{12,28},{16,0},{20,4},{24,8},{28,12},{32,48},... | collective-permute-start | bytes 196616 | tf_op jit(solution)/shard_map/ppermute | solution.py:29
  78.8 16.0 %copy-start.20 = (f32[16,32,32]{1,2,0:T(8,128)S(1)}, f32[16,32,32]{1,2,0:T(8,128)}, u32[]{:S(2)}) copy-start(f32[16,32,32]{1,2,0:T(8,128)} %get-tuple-element.96) | copy-start | bytes 196612
  78.8 16.0 %copy-start.21 = (f32[16,32,32]{1,2,0:T(8,128)S(1)}, f32[16,32,32]{1,2,0:T(8,128)}, u32[]{:S(2)}) copy-start(f32[16,32,32]{1,2,0:T(8,128)} %get-tuple-element.97) | copy-start | bytes 196612
  78.8 16.0 %copy-start.22 = (f32[16,32,32]{1,2,0:T(8,128)S(1)}, f32[16,32,32]{1,2,0:T(8,128)}, u32[]{:S(2)}) copy-start(f32[16,32,32]{1,2,0:T(8,128)} %get-tuple-element.98) | copy-start | bytes 196612
  78.8 16.0 %copy-start.23 = (f32[16,32,32]{1,2,0:T(8,128)S(1)}, f32[16,32,32]{1,2,0:T(8,128)}, u32[]{:S(2)}) copy-start(f32[16,32,32]{1,2,0:T(8,128)} %get-tuple-element.99) | copy-start | bytes 196612
  78.8 16.0 %copy-start.24 = (f32[16,32,32]{1,2,0:T(8,128)S(1)}, f32[16,32,32]{1,2,0:T(8,128)}, u32[]{:S(2)}) copy-start(f32[16,32,32]{1,2,0:T(8,128)} %get-tuple-element.100) | copy-start | bytes 196612
  78.8 16.0 %copy-start.25 = (f32[16,32,32]{1,2,0:T(8,128)S(1)}, f32[16,32,32]{1,2,0:T(8,128)}, u32[]{:S(2)}) copy-start(f32[16,32,32]{1,2,0:T(8,128)} %get-tuple-element.101) | copy-start | bytes 196612
  78.9 15.9 %collective-permute-start.5 = (f32[16,16,64]{2,0,1:T(8,128)S(1)}, f32[16,16,64]{2,0,1:T(8,128)S(1)}, u32[]{:S(2)}, u32[]{:S(2)}) collective-permute-start(f32[16,16,64]{2,0,1:T(8,128)S(1)} %convolution_bitcast_fusion.5), channel_id=1, source_target_pairs={{0,32},{4,36},{8,40},{12,44},{16,48},{20,52},{24,56},{28,60},{32,0... | collective-permute-start | bytes 196616 | tf_op jit(solution)/shard_map/ppermute | solution.py:29
  94.8 11.3 %copy-start.14 = (f32[16,32,32]{1,2,0:T(8,128)S(1)}, f32[16,32,32]{1,2,0:T(8,128)}, u32[]{:S(2)}) copy-start(f32[16,32,32]{1,2,0:T(8,128)} %get-tuple-element.102) | copy-start | bytes 196612
  94.8 11.3 %copy-start.15 = (f32[16,32,32]{1,2,0:T(8,128)S(1)}, f32[16,32,32]{1,2,0:T(8,128)}, u32[]{:S(2)}) copy-start(f32[16,32,32]{1,2,0:T(8,128)} %get-tuple-element.103) | copy-start | bytes 196612
  94.8 11.3 %copy-start.16 = (f32[16,32,32]{1,2,0:T(8,128)S(1)}, f32[16,32,32]{1,2,0:T(8,128)}, u32[]{:S(2)}) copy-start(f32[16,32,32]{1,2,0:T(8,128)} %get-tuple-element.104) | copy-start | bytes 196612
  94.9 11.3 %copy-start.17 = (f32[16,32,32]{1,2,0:T(8,128)S(1)}, f32[16,32,32]{1,2,0:T(8,128)}, u32[]{:S(2)}) copy-start(f32[16,32,32]{1,2,0:T(8,128)} %get-tuple-element.105) | copy-start | bytes 196612
  94.9 11.3 %copy-start.18 = (f32[16,32,32]{1,2,0:T(8,128)S(1)}, f32[16,32,32]{1,2,0:T(8,128)}, u32[]{:S(2)}) copy-start(f32[16,32,32]{1,2,0:T(8,128)} %get-tuple-element.106) | copy-start | bytes 196612
  94.9 11.3 %copy-start.19 = (f32[16,32,32]{1,2,0:T(8,128)S(1)}, f32[16,32,32]{1,2,0:T(8,128)}, u32[]{:S(2)}) copy-start(f32[16,32,32]{1,2,0:T(8,128)} %get-tuple-element.107) | copy-start | bytes 196612
  96.2 9.9 %collective-permute-start.6 = (f32[16,16,64]{2,0,1:T(8,128)S(1)}, f32[16,16,64]{2,0,1:T(8,128)S(1)}, u32[]{:S(2)}, u32[]{:S(2)}) collective-permute-start(f32[16,16,64]{2,0,1:T(8,128)S(1)} %convolution_bitcast_fusion.4), channel_id=1, source_target_pairs={{0,64},{4,68},{8,72},{12,76},{16,80},{20,84},{24,88},{28,92},{32,9... | collective-permute-start | bytes 196616 | tf_op jit(solution)/shard_map/ppermute | solution.py:29
  98.2 15.2 %collective-permute-start.11 = (f32[32,4,128]{2,0,1:T(8,128)S(1)}, f32[32,4,128]{2,0,1:T(8,128)S(1)}, u32[]{:S(2)}, u32[]{:S(2)}) collective-permute-start(f32[32,4,128]{2,0,1:T(8,128)S(1)} %get-tuple-element.123), channel_id=1, source_target_pairs={{0,1},{1,2},{2,3},{3,4},{4,5},{5,6},{6,7},{7,8},{8,9},{9,10},{10,1... | collective-permute-start | bytes 196616 | tf_op jit(solution)/shard_map/ppermute | solution.py:35
  100.9 19.0 %copy-start.8 = (f32[16,32,32]{1,2,0:T(8,128)S(1)}, f32[16,32,32]{1,2,0:T(8,128)}, u32[]{:S(2)}) copy-start(f32[16,32,32]{1,2,0:T(8,128)} %get-tuple-element.108) | copy-start | bytes 196612
  100.9 19.0 %copy-start.9 = (f32[16,32,32]{1,2,0:T(8,128)S(1)}, f32[16,32,32]{1,2,0:T(8,128)}, u32[]{:S(2)}) copy-start(f32[16,32,32]{1,2,0:T(8,128)} %get-tuple-element.109) | copy-start | bytes 196612
  101.0 19.0 %copy-start.10 = (f32[16,32,32]{1,2,0:T(8,128)S(1)}, f32[16,32,32]{1,2,0:T(8,128)}, u32[]{:S(2)}) copy-start(f32[16,32,32]{1,2,0:T(8,128)} %get-tuple-element.110) | copy-start | bytes 196612
  101.0 19.0 %copy-start.11 = (f32[16,32,32]{1,2,0:T(8,128)S(1)}, f32[16,32,32]{1,2,0:T(8,128)}, u32[]{:S(2)}) copy-start(f32[16,32,32]{1,2,0:T(8,128)} %get-tuple-element.111) | copy-start | bytes 196612
  101.0 19.0 %copy-start.12 = (f32[16,32,32]{1,2,0:T(8,128)S(1)}, f32[16,32,32]{1,2,0:T(8,128)}, u32[]{:S(2)}) copy-start(f32[16,32,32]{1,2,0:T(8,128)} %get-tuple-element.112) | copy-start | bytes 196612
  101.0 19.0 %copy-start.13 = (f32[16,32,32]{1,2,0:T(8,128)S(1)}, f32[16,32,32]{1,2,0:T(8,128)}, u32[]{:S(2)}) copy-start(f32[16,32,32]{1,2,0:T(8,128)} %get-tuple-element.113) | copy-start | bytes 196612
  101.0 29.0 %collective-permute-start.12 = (f32[32,4,128]{2,0,1:T(8,128)S(1)}, f32[32,4,128]{2,0,1:T(8,128)S(1)}, u32[]{:S(2)}, u32[]{:S(2)}) collective-permute-start(f32[32,4,128]{2,0,1:T(8,128)S(1)} %get-tuple-element.122), channel_id=1, source_target_pairs={{0,511},{1,0},{2,1},{3,2},{4,3},{5,4},{6,5},{7,6},{8,7},{9,8},{10,... | collective-permute-start | bytes 196616 | tf_op jit(solution)/shard_map/ppermute | solution.py:35
  107.4 12.5 %collective-permute-start.7 = (f32[16,16,64]{2,0,1:T(8,128)S(1)}, f32[16,16,64]{2,0,1:T(8,128)S(1)}, u32[]{:S(2)}, u32[]{:S(2)}) collective-permute-start(f32[16,16,64]{2,0,1:T(8,128)S(1)} %convolution_bitcast_fusion.3), channel_id=1, source_target_pairs={{0,128},{4,132},{8,136},{12,140},{16,144},{20,148},{24,152},{28,15... | collective-permute-start | bytes 196616 | tf_op jit(solution)/shard_map/ppermute | solution.py:29
  113.3 23.1 %copy-start.6 = (f32[16,32,32]{1,2,0:T(8,128)S(1)}, f32[16,32,32]{1,2,0:T(8,128)}, u32[]{:S(2)}) copy-start(f32[16,32,32]{1,2,0:T(8,128)} %get-tuple-element.118) | copy-start | bytes 196612
  113.3 23.1 %copy-start.7 = (f32[16,32,32]{1,2,0:T(8,128)S(1)}, f32[16,32,32]{1,2,0:T(8,128)}, u32[]{:S(2)}) copy-start(f32[16,32,32]{1,2,0:T(8,128)} %get-tuple-element.119) | copy-start | bytes 196612
  121.3 15.1 %collective-permute-start.8 = (f32[16,16,64]{2,0,1:T(8,128)S(1)}, f32[16,16,64]{2,0,1:T(8,128)S(1)}, u32[]{:S(2)}, u32[]{:S(2)}) collective-permute-start(f32[16,16,64]{2,0,1:T(8,128)S(1)} %convolution_bitcast_fusion.2), channel_id=1, source_target_pairs={{0,256},{4,260},{8,264},{12,268},{16,272},{20,276},{24,280},{28,28... | collective-permute-start | bytes 196616 | tf_op jit(solution)/shard_map/ppermute | solution.py:29
  (17 other events, 41.5 us)
where the time goes:
time: 140 us
  starting transfers between devices  59.1 us (42%)
  waiting for transfers between devices  30.7 us (22%)
  matrix products  21.4 us (15%)
  other arithmetic  17.4 us (12%)
  local copies, waits for them, and re-layouts  9.43 us (7%)
  between operations  1.5 us (1%)
    ppermute x9, starting transfers between devices, swapped(): lax.ppermute(shard, axis, [(i, i ^ 1 << distance) for i in range(lax.axis...  45.5 us
    ppermute x9, waiting for transfers between devices, swapped(): lax.ppermute(shard, axis, [(i, i ^ 1 << distance) for i in range(lax.axis...  30.7 us
    dot_general x13, matrix products, apply_level(): jnp.einsum('rsm,smn->rsn', paired, block_form(weights), precision=highest)  19 us
    neg x13, other arithmetic, block_form(): upper_rows = jnp.concatenate([real_part, -imag_part], axis=2)  11.7 us
    ppermute x2, starting transfers between devices, from_behind(): return lax.ppermute(value, axis, pairs)  7.8 us
    unnamed x120, local copies, waits for them, and re-layouts  6.89 us
    ppermute x1, starting transfers between devices, with_halo(): lax.ppermute(head, axis, [((i + 1) % count, i) for i in range(count)])  3.94 us
  transfers between devices with their start and end apart: 13, of which 7 were waited for; matrix products, arithmetic and copies ran while one was open for 16% of the time, Pallas kernels for 0%

commit v1 on v0

v1 whole, which is shorter than its diff:
```python
import functools

import jax
import jax.numpy as jnp
from jax import lax
from jax.experimental import pallas as pl
from jax.experimental.pallas import tpu as pltpu
from jax.sharding import PartitionSpec as P

LEAF = 128
BOXES = 16
PAIRS = 8
RHS = 16
CAP = 24
REACH = 4
LEVELS = 13
LOCAL = 4
PHASES = (
    ("sub", (0, 1)),
    ("leaf", (0,)),
    ("leaf", (1,)),
    ("leaf", (2, 3)),
    ("leaf", (4,)),
    ("leaf", (5, 6)),
)
WIRE = "f32"

BF = jnp.bfloat16
F32 = jnp.float32
MESH = pl.DeviceIdType.MESH


def bit_of(index, bit):
    return (index // (1 << bit)) % 2


def flipped(index, bit):
    return index + (1 - 2 * bit_of(index, bit)) * (1 << bit)


def pieces(values):
    high = values.astype(BF)
    low = (values - high.astype(F32)).astype(BF)
    return jnp.concatenate([high, low], axis=0)


def folded(product):
    half = product.shape[0] // 2
    return product[:half] + product[half:]


def dot(left, right):
    return jnp.dot(left, right, preferred_element_type=F32)


def phase_plan():
    plan = []
    level = LOCAL
    slot = 0
    for axis, bits in PHASES:
        if len(bits) == 1:
            plan.append((axis, bits, level, ((bits[0],),), None))
        else:
            low, high = bits
            plan.append((axis, bits, level, ((high,), (low, high), (low,)), slot))
            slot += 1
        level += len(bits)
    return tuple(plan), slot


PLAN, MERGED = phase_plan()
PARTNERS = sum(len(entry[3]) for entry in PLAN)


def kernel(
    list_ref, sig_hbm, row_hbm, tr_hbm, col_hbm, near_hbm, out_hbm,
    sig, row, tr, col, near, window, mats, far_tr, far_mats, basis, send_buf, recv_buf,
    products, field, rim, out, load_sem, push_sem, pull_sem, store_sem,
):
    leaf = lax.axis_index("leaf")
    sub = lax.axis_index("sub")
    leaves = lax.axis_size("leaf")
    subs = lax.axis_size("sub")

    loads = [
        pltpu.make_async_copy(sig_hbm, sig, load_sem.at[0]),
        pltpu.make_async_copy(row_hbm, row, load_sem.at[1]),
        pltpu.make_async_copy(tr_hbm.at[:, :LOCAL], tr.at[:, :LOCAL], load_sem.at[2]),
        pltpu.make_async_copy(tr_hbm.at[:, LOCAL:], tr.at[:, LOCAL:], load_sem.at[3]),
        pltpu.make_async_copy(near_hbm, near, load_sem.at[4]),
        pltpu.make_async_copy(col_hbm, col, load_sem.at[5]),
    ]
    for load in loads:
        load.start()

    def partner(axis, bits):
        place = leaf if axis == "leaf" else sub
        for bit in bits:
            place = flipped(place, bit)
        return (place, sub) if axis == "leaf" else (leaf, place)

    rank = leaf * subs + sub
    after = (rank + 1) % (leaves * subs)
    before = (rank + leaves * subs - 1) % (leaves * subs)
    after = (after // subs, after % subs)
    before = (before // subs, before % subs)

    peers = [partner(axis, bits) for axis, _, _, sets, _ in PLAN for bits in sets]
    peers += [after, before]
    barrier = pltpu.get_barrier_semaphore()
    for peer in peers:
        pl.semaphore_signal(barrier, inc=1, device_id=peer, device_id_type=MESH)

    lane = lax.broadcasted_iota(jnp.int32, (32, LEAF), 1)
    group = lane // 32
    odd = (group % 2).astype(F32)
    upper = (group // 2).astype(F32)
    odd_b = odd.astype(BF)
    even_b = (1.0 - odd).astype(BF)
    sign_b = (1.0 - 2.0 * odd).astype(BF)
    upper_b = upper.astype(BF)
    lower_b = (1.0 - upper).astype(BF)
    first_half = lax.broadcasted_iota(jnp.int32, (RHS, LEAF), 1) < 64

    def turned(weights):
        signed = weights * sign_b
        crossed = pltpu.roll(weights, 96, 1) * even_b + pltpu.roll(weights, 32, 1) * odd_b
        return signed, crossed, pltpu.roll(signed, 64, 1), pltpu.roll(crossed, 64, 1)

    def expand(source, target):
        def body(pair, carry):
            s0, c0, sr0, cr0 = turned(source(2 * pair))
            s1, c1, sr1, cr1 = turned(source(2 * pair + 1))
            target[pair, 0] = jnp.concatenate(
                [s0 * lower_b, c0 * lower_b, sr1 * upper_b, cr1 * upper_b], axis=0
            )
            target[pair, 1] = jnp.concatenate(
                [sr0 * lower_b, cr0 * lower_b, s1 * upper_b, c1 * upper_b], axis=0
            )
            return carry

        lax.fori_loop(0, PAIRS, body, 0)

    def expand_first(source, target):
        def body(pair, carry):
            s0, c0, sr0, cr0 = turned(source(2 * pair))
            s1, c1, sr1, cr1 = turned(source(2 * pair + 1))
            target[pair, 0] = jnp.concatenate(
                [
                    s0 * lower_b + sr1 * upper_b,
                    c0 * lower_b + cr1 * upper_b,
                    sr0 * lower_b + s1 * upper_b,
                    cr0 * lower_b + c1 * upper_b,
                ],
                axis=0,
            )
            return carry

        lax.fori_loop(0, PAIRS, body, 0)

    def expand_level(level):
        expand(lambda box: tr[box, level], mats.at[level])

    loads[0].wait()
    loads[1].wait()
    coeffs = []
    for pair in range(PAIRS):
        left, right = [], []
        for box in (2 * pair, 2 * pair + 1):
            points = slice(box * LEAF, (box + 1) * LEAF)
            samples = sig[:, points]
            window[2 * REACH + box] = samples
            left.append(jnp.concatenate([samples[:RHS], samples[RHS:]], axis=1))
            real, imag = row[:32, points], row[32:, points]
            right.append(
                jnp.concatenate(
                    [jnp.concatenate([real, imag], axis=1), jnp.concatenate([-imag, real], axis=1)],
                    axis=0,
                )
            )
        product = lax.dot_general(
            jnp.concatenate(left, axis=0), jnp.concatenate(right, axis=0),
            (((1,), (1,)), ((), ())), preferred_element_type=F32,
        )
        coeffs.append(jnp.where(first_half, product[:RHS], product[RHS:]))

    loads[2].wait()
    expand_first(lambda box: tr[box, 0], mats.at[0])
    for level in range(1, LOCAL):
        expand_level(level)
    loads[3].wait()
    pl.semaphore_wait(barrier, len(peers))

    pushes = []

    def remote(source, target, number, peer):
        return pltpu.make_async_remote_copy(
            src_ref=source, dst_ref=target, send_sem=push_sem.at[number],
            recv_sem=pull_sem.at[number], device_id=peer, device_id_type=MESH,
        )

    weight_copies = {}
    for axis, bits, level, sets, slot in PLAN:
        if slot is not None:
            copy = remote(tr.at[:, level], far_tr.at[slot], PARTNERS + slot, partner(axis, sets[0]))
            copy.start()
            pushes.append(copy)
            weight_copies[slot] = copy

    coeffs = [folded(dot(pieces(coeffs[pair]), mats[0, pair, 0])) for pair in range(PAIRS)]
    for level in range(1, LOCAL):
        span = 1 << (level - 1)
        split = [pieces(values) for values in coeffs]
        following = []
        for pair in range(PAIRS):
            low = pair & ~span
            joined = jnp.concatenate([split[low], split[low | span]], axis=1)
            weights = mats[level, pair].reshape(2 * LEAF, LEAF)
            following.append(folded(dot(joined, weights)))
        coeffs = following

    edge = 2 * REACH
    halo = (
        remote(window.at[BOXES : BOXES + edge], window.at[:edge], PARTNERS + MERGED, after),
        remote(window.at[edge : 2 * edge], window.at[edge + BOXES :], PARTNERS + MERGED + 1, before),
    )

    def send_halo():
        for copy in halo:
            copy.start()
            pushes.append(copy)

    def near_field():
        for copy in halo:
            copy.wait_recv()
        loads[4].wait()

        def multiply(slot, carry):
            picked = window[jnp.maximum(list_ref[slot, 0], 0)]
            product = dot(picked, near[slot])
            real = product[:RHS, :LEAF] + product[RHS:, LEAF:]
            imag = product[RHS:, :LEAF] - product[:RHS, LEAF:]
            products[slot] = jnp.concatenate([real, imag], axis=0)
            return carry

        lax.fori_loop(0, CAP, multiply, 0)

        def gather(box, carry):
            total = jnp.zeros((2 * RHS, LEAF), F32)
            for slot in range(CAP):
                here = jnp.where(list_ref[slot, 1] == box, 1.0, 0.0).astype(F32)
                total += products[slot] * here
            field[box] = total
            return carry

        lax.fori_loop(0, BOXES + 2 * REACH, gather, 0)

    rims = (
        remote(field.at[:REACH], rim.at[0], PARTNERS + MERGED + 2, before),
        remote(field.at[BOXES + REACH :], rim.at[1], PARTNERS + MERGED + 3, after),
    )

    def send_rims():
        for copy in rims:
            copy.start()
            pushes.append(copy)

    def expand_basis():
        loads[5].wait()
        for box in range(BOXES):
            points = slice(box * LEAF, (box + 1) * LEAF)
            real, imag = col[:32, points], col[32:, points]
            basis[box // 2, 64 * (box % 2) : 64 * (box % 2) + 64] = jnp.concatenate(
                [jnp.concatenate([real, imag], axis=1), jnp.concatenate([-imag, real], axis=1)],
                axis=0,
            )

    def expand_far(slot):
        weight_copies[slot].wait_recv()
        expand(lambda box: far_tr[slot, box], far_mats.at[slot])

    fillers = [
        [lambda: expand_level(4), lambda: expand_level(5), lambda: expand_level(6),
         lambda: expand_level(7)],
        [],
        [lambda: expand_level(8), lambda: expand_level(9), near_field, send_rims],
        [lambda: expand_far(1), lambda: expand_level(10), lambda: expand_level(11),
         lambda: expand_level(12), expand_basis],
        [lambda: expand_far(2)],
        [],
    ]

    number = 0
    for step, (axis, bits, level, sets, slot) in enumerate(PLAN):
        place = leaf if axis == "leaf" else sub
        for pair in range(PAIRS):
            send_buf[step, RHS * pair : RHS * (pair + 1)] = coeffs[pair]
        copies = []
        for partner_bits in sets:
            copy = remote(
                send_buf.at[step], recv_buf.at[number], number, partner(axis, partner_bits)
            )
            copy.start()
            copies.append(copy)
            number += 1
        pushes.extend(copies)
        if step == 0:
            send_halo()
            for level_now in (4, 5):
                expand_level(level_now)
            fill = [lambda: expand_level(6), lambda: expand_level(7), lambda: expand_far(0)]
        else:
            fill = fillers[step]
        mine = bit_of(place, bits[0])
        other = 1 - mine
        partial = [
            folded(dot(pieces(coeffs[pair]), mats[level, pair, mine])) for pair in range(PAIRS)
        ]
        for task in fill:
            task()
        first = number - len(sets)

        def block(index, pair):
            return recv_buf[index, RHS * pair : RHS * (pair + 1)]

        copies[-1].wait_recv()
        coeffs = [
            partial[pair]
            + folded(dot(pieces(block(number - 1, pair)), mats[level, pair, other]))
            for pair in range(PAIRS)
        ]
        if len(bits) == 2:
            copies[0].wait_recv()
            far = [
                folded(dot(pieces(block(first, pair)), far_mats[slot, pair, mine]))
                for pair in range(PAIRS)
            ]
            mine_next = bit_of(place, bits[1])
            partial = [
                folded(dot(pieces(coeffs[pair]), mats[level + 1, pair, mine_next]))
                for pair in range(PAIRS)
            ]
            copies[1].wait_recv()
            far = [
                far[pair]
                + folded(dot(pieces(block(first + 1, pair)), far_mats[slot, pair, other]))
                for pair in range(PAIRS)
            ]
            coeffs = [
                partial[pair]
                + folded(dot(pieces(far[pair]), mats[level + 1, pair, 1 - mine_next]))
                for pair in range(PAIRS)
            ]

    for copy in rims:
        copy.wait_recv()
    for place in range(REACH):
        field[REACH + place] += rim[1, place]
        field[BOXES + place] += rim[0, place]

    stores = []
    for pair in range(PAIRS):
        values = coeffs[pair]
        zero = jnp.zeros_like(values)
        left = jnp.concatenate(
            [pieces(jnp.where(first_half, values, zero)), pieces(jnp.where(first_half, zero, values))],
            axis=0,
        )
        product = dot(left, basis[pair])
        for half in range(2):
            far_box = folded(product[2 * RHS * half : 2 * RHS * (half + 1)])
            box = 2 * pair + half
            points = slice(box * LEAF, (box + 1) * LEAF)
            near_box = field[REACH + box]
            out[:RHS, points] = far_box[:, :LEAF] + near_box[:RHS]
            out[RHS:, points] = far_box[:, LEAF:] + near_box[RHS:]
        points = slice(2 * pair * LEAF, (2 * pair + 2) * LEAF)
        store = pltpu.make_async_copy(out.at[:, points], out_hbm.at[:, points], store_sem.at[pair])
        store.start()
        stores.append(store)
    for copy in pushes:
        copy.wait_send()
    for store in stores:
        store.wait()


def shards(signal, row_basis, transfer, column_basis, near_blocks, near_list):
    anywhere = pl.BlockSpec(memory_space=pl.ANY)
    copies = PARTNERS + MERGED + 4
    return pl.pallas_call(
        kernel,
        out_shape=jax.ShapeDtypeStruct((2 * RHS, BOXES * LEAF), F32),
        in_specs=[pl.BlockSpec(memory_space=pltpu.SMEM)] + [anywhere] * 5,
        out_specs=anywhere,
        scratch_shapes=[
            pltpu.VMEM((2 * RHS, BOXES * LEAF), BF),
            pltpu.VMEM((64, BOXES * LEAF), BF),
            pltpu.VMEM((BOXES, LEVELS, 32, LEAF), BF),
            pltpu.VMEM((64, BOXES * LEAF), BF),
            pltpu.VMEM((CAP, LEAF, 2 * LEAF), BF),
            pltpu.VMEM((BOXES + 4 * REACH, 2 * RHS, LEAF), BF),
            pltpu.VMEM((LEVELS, PAIRS, 2, LEAF, LEAF), BF),
            pltpu.VMEM((MERGED, BOXES, 32, LEAF), BF),
            pltpu.VMEM((MERGED, PAIRS, 2, LEAF, LEAF), BF),
            pltpu.VMEM((PAIRS, LEAF, 2 * LEAF), BF),
            pltpu.VMEM((len(PLAN), PAIRS * RHS, LEAF), F32),
            pltpu.VMEM((PARTNERS, PAIRS * RHS, LEAF), F32),
            pltpu.VMEM((CAP, 2 * RHS, LEAF), F32),
            pltpu.VMEM((BOXES + 2 * REACH, 2 * RHS, LEAF), F32),
            pltpu.VMEM((2, REACH, 2 * RHS, LEAF), F32),
            pltpu.VMEM((2 * RHS, BOXES * LEAF), F32),
            pltpu.SemaphoreType.DMA((6,)),
            pltpu.SemaphoreType.DMA((copies,)),
            pltpu.SemaphoreType.DMA((copies,)),
            pltpu.SemaphoreType.DMA((PAIRS,)),
        ],
        compiler_params=pltpu.CompilerParams(
            collective_id=0, has_side_effects=True, vmem_limit_bytes=56 * 1024 * 1024
        ),
        name="adjoint",
    )(near_list, signal, row_basis, transfer, column_basis, near_blocks)


def solution(mesh):
    return jax.shard_map(
        shards,
        mesh=mesh,
        in_specs=(
            P(None, ("leaf", "sub")),
            P(None, ("leaf", "sub")),
            P(("leaf", "sub"), None, None, None),
            P(None, ("leaf", "sub")),
            P(("leaf", "sub"), None, None),
            P(("leaf", "sub"), None),
        ),
        out_specs=P(None, ("leaf", "sub")),
        check_vma=False,
    )
```

time: 140 us -> 61.5 us (0.44)
  the two profiles are of different devices: /device:TPU:56 before, /device:TPU:1 now
where the time goes in v1:
time: 61.5 us; the launch traced here: 61.3 us
  Pallas kernels  58.2 us (95%)
  local copies, waits for them, and re-layouts  3.03 us (5%)
    pallas_call x1, Pallas kernels, shards(): pl.pallas_call(kernel, out_shape=jax.ShapeDtypeStruct((2 * RHS, BOXES * L...  58.2 us
    unnamed x2, local copies, waits for them, and re-layouts  3.03 us

profile of v1, /device:TPU:1, one launch (start us, length us, event | category | flops | bytes accessed | tf_op | source)
XLA Modules:
  0.0 61.3 jit_solution(275145974187885008)
XLA Ops:
  0.0 1.4 %copy.7.list_ref = s32[24,2]{1,0:T(8,128)} copy(s32[24,2]{0,1:T(2,128)} %param.11) | data formatting | bytes 384 | tf_op args[5]
  1.4 58.2 %adjoint.1 = f32[32,2048]{1,0:T(8,128)} custom-call(s32[24,2]{1,0:T(8,128)} %copy.7.list_ref, bf16[32,2048]{1,0:T(8,128)(2,1)} %sig_hbm.1, bf16[64,2048]{1,0:T(8,128)(2,1)} %row_hbm.1, bf16[16,13,32,128]{3,2,1,0:T(8,128)(2,1)} %tr_hbm.1, bf16[64,2048]{1,0:T(8,128)(2,1)} %col_hbm.1, bf16[24,128,256]{2,1,0:T(8,128)(2,1)} %near_hbm.1), custom_call_target="tpu_custom_call" | custom-call | tf_op jit(solution)/shard_map/adjoint/pallas_call | solution.py:390
  59.6 1.7 %copy.9 = f32[32,2048]{1,0:T(8,128)} copy(f32[32,2048]{1,0:T(8,128)} %adjoint.1) | data formatting | bytes 524288

commit v2 on v1

--- a/solution.py
+++ b/solution.py
@@ -23,7 +23,8 @@
     ("leaf", (4,)),
     ("leaf", (5, 6)),
 )
-WIRE = "f32"
+FULL = 32767.0
+SMALLEST = 1e-30
 
 BF = jnp.bfloat16
 F32 = jnp.float32
@@ -51,6 +52,17 @@
 
 def dot(left, right):
     return jnp.dot(left, right, preferred_element_type=F32)
+
+
+def coded(coeffs):
+    peak = jnp.abs(coeffs[0])
+    for values in coeffs[1:]:
+        peak = jnp.maximum(peak, jnp.abs(values))
+    peak = jnp.maximum(jnp.maximum(peak[:8], peak[8:]), SMALLEST)
+    inverse = FULL / peak
+    inverse = jnp.concatenate([inverse, inverse], axis=0)
+    codes = [jnp.round(values * inverse).astype(jnp.int32).astype(jnp.int16) for values in coeffs]
+    return codes, peak * (1.0 / FULL)
 
 
 def phase_plan():
@@ -70,12 +82,13 @@
 
 PLAN, MERGED = phase_plan()
 PARTNERS = sum(len(entry[3]) for entry in PLAN)
+SCALES = PARTNERS + MERGED + 4
 
 
 def kernel(
-    list_ref, sig_hbm, row_hbm, tr_hbm, col_hbm, near_hbm, out_hbm,
-    sig, row, tr, col, near, window, mats, far_tr, far_mats, basis, send_buf, recv_buf,
-    products, field, rim, out, load_sem, push_sem, pull_sem, store_sem,
+    list_ref, sig_hbm, row_hbm, tr_hbm, col_hbm, near_hbm, out,
+    sig, row, tr, col, near, window, mats, far_tr, far_mats, basis, send_buf, recv_buf, send_scale, recv_scale,
+    products, field, rim, load_sem, push_sem, pull_sem,
 ):
     leaf = lax.axis_index("leaf")
     sub = lax.axis_index("sub")
@@ -123,9 +136,13 @@
     first_half = lax.broadcasted_iota(jnp.int32, (RHS, LEAF), 1) < 64
 
     def turned(weights):
-        signed = weights * sign_b
-        crossed = pltpu.roll(weights, 96, 1) * even_b + pltpu.roll(weights, 32, 1) * odd_b
-        return signed, crossed, pltpu.roll(signed, 64, 1), pltpu.roll(crossed, 64, 1)
+        by32, by64, by96 = (pltpu.roll(weights, shift, 1) for shift in (32, 64, 96))
+        return (
+            weights * sign_b,
+            by96 * even_b + by32 * odd_b,
+            by64 * sign_b,
+            by32 * even_b + by96 * odd_b,
+        )
 
     def expand(source, target):
         def body(pair, carry):
@@ -139,7 +156,7 @@
             )
             return carry
 
-        lax.fori_loop(0, PAIRS, body, 0)
+        lax.fori_loop(0, PAIRS, body, 0, unroll=8)
 
     def expand_first(source, target):
         def body(pair, carry):
@@ -156,7 +173,7 @@
             )
             return carry
 
-        lax.fori_loop(0, PAIRS, body, 0)
+        lax.fori_loop(0, PAIRS, body, 0, unroll=8)
 
     def expand_level(level):
         expand(lambda box: tr[box, level], mats.at[level])
@@ -236,19 +253,19 @@
         loads[4].wait()
 
         def multiply(slot, carry):
-            picked = window[jnp.maximum(list_ref[slot, 0], 0)]
+            picked = window[jnp.maximum(list_ref[0, slot], 0)]
             product = dot(picked, near[slot])
             real = product[:RHS, :LEAF] + product[RHS:, LEAF:]
             imag = product[RHS:, :LEAF] - product[:RHS, LEAF:]
             products[slot] = jnp.concatenate([real, imag], axis=0)
             return carry
 
-        lax.fori_loop(0, CAP, multiply, 0)
+        lax.fori_loop(0, CAP, multiply, 0, unroll=8)
 
         def gather(box, carry):
             total = jnp.zeros((2 * RHS, LEAF), F32)
             for slot in range(CAP):
-                here = jnp.where(list_ref[slot, 1] == box, 1.0, 0.0).astype(F32)
+                here = jnp.where(list_ref[1, slot] == box, 1.0, 0.0).astype(F32)
                 total += products[slot] * here
             field[box] = total
             return carry
@@ -293,17 +310,22 @@
     number = 0
     for step, (axis, bits, level, sets, slot) in enumerate(PLAN):
         place = leaf if axis == "leaf" else sub
+        codes, scale = coded(coeffs)
         for pair in range(PAIRS):
-            send_buf[step, RHS * pair : RHS * (pair + 1)] = coeffs[pair]
+            send_buf[step, RHS * pair : RHS * (pair + 1)] = codes[pair]
+        send_scale[step] = scale
         copies = []
         for partner_bits in sets:
-            copy = remote(
-                send_buf.at[step], recv_buf.at[number], number, partner(axis, partner_bits)
-            )
-            copy.start()
-            copies.append(copy)
+            peer = partner(axis, partner_bits)
+            both = (
+                remote(send_scale.at[step], recv_scale.at[number], SCALES + number, peer),
+                remote(send_buf.at[step], recv_buf.at[number], number, peer),
+            )
+            for copy in both:
+                copy.start()
+            pushes.extend(both)
+            copies.append(both)
             number += 1
-        pushes.extend(copies)
         if step == 0:
             send_halo()
             for level_now in (4, 5):
@@ -321,16 +343,22 @@
         first = number - len(sets)
 
         def block(index, pair):
-            return recv_buf[index, RHS * pair : RHS * (pair + 1)]
-
-        copies[-1].wait_recv()
+            scale = recv_scale[index]
+            scale = jnp.concatenate([scale, scale], axis=0)
+            return recv_buf[index, RHS * pair : RHS * (pair + 1)].astype(F32) * scale
+
+        def arrived(both):
+            for copy in both:
+                copy.wait_recv()
+
+        arrived(copies[-1])
         coeffs = [
             partial[pair]
             + folded(dot(pieces(block(number - 1, pair)), mats[level, pair, other]))
             for pair in range(PAIRS)
         ]
         if len(bits) == 2:
-            copies[0].wait_recv()
+            arrived(copies[0])
             far = [
                 folded(dot(pieces(block(first, pair)), far_mats[slot, pair, mine]))
                 for pair in range(PAIRS)
@@ -340,7 +368,7 @@
                 folded(dot(pieces(coeffs[pair]), mats[level + 1, pair, mine_next]))
                 for pair in range(PAIRS)
             ]
-            copies[1].wait_recv()
+            arrived(copies[1])
             far = [
                 far[pair]
                 + folded(dot(pieces(block(first + 1, pair)), far_mats[slot, pair, other]))
@@ -358,7 +386,6 @@
         field[REACH + place] += rim[1, place]
         field[BOXES + place] += rim[0, place]
 
-    stores = []
     for pair in range(PAIRS):
         values = coeffs[pair]
         zero = jnp.zeros_like(values)
@@ -374,24 +401,18 @@
             near_box = field[REACH + box]
             out[:RHS, points] = far_box[:, :LEAF] + near_box[:RHS]
             out[RHS:, points] = far_box[:, LEAF:] + near_box[RHS:]
-        points = slice(2 * pair * LEAF, (2 * pair + 2) * LEAF)
-        store = pltpu.make_async_copy(out.at[:, points], out_hbm.at[:, points], store_sem.at[pair])
-        store.start()
-        stores.append(store)
     for copy in pushes:
         copy.wait_send()
-    for store in stores:
-        store.wait()
 
 
 def shards(signal, row_basis, transfer, column_basis, near_blocks, near_list):
     anywhere = pl.BlockSpec(memory_space=pl.ANY)
-    copies = PARTNERS + MERGED + 4
+    copies = SCALES + PARTNERS
     return pl.pallas_call(
         kernel,
         out_shape=jax.ShapeDtypeStruct((2 * RHS, BOXES * LEAF), F32),
         in_specs=[pl.BlockSpec(memory_space=pltpu.SMEM)] + [anywhere] * 5,
-        out_specs=anywhere,
+        out_specs=pl.BlockSpec(memory_space=pltpu.VMEM),
         scratch_shapes=[
             pltpu.VMEM((2 * RHS, BOXES * LEAF), BF),
             pltpu.VMEM((64, BOXES * LEAF), BF),
@@ -403,22 +424,22 @@
             pltpu.VMEM((MERGED, BOXES, 32, LEAF), BF),
             pltpu.VMEM((MERGED, PAIRS, 2, LEAF, LEAF), BF),
             pltpu.VMEM((PAIRS, LEAF, 2 * LEAF), BF),
-            pltpu.VMEM((len(PLAN), PAIRS * RHS, LEAF), F32),
-            pltpu.VMEM((PARTNERS, PAIRS * RHS, LEAF), F32),
+            pltpu.VMEM((len(PLAN), PAIRS * RHS, LEAF), jnp.int16),
+            pltpu.VMEM((PARTNERS, PAIRS * RHS, LEAF), jnp.int16),
+            pltpu.VMEM((len(PLAN), 8, LEAF), F32),
+            pltpu.VMEM((PARTNERS, 8, LEAF), F32),
             pltpu.VMEM((CAP, 2 * RHS, LEAF), F32),
             pltpu.VMEM((BOXES + 2 * REACH, 2 * RHS, LEAF), F32),
             pltpu.VMEM((2, REACH, 2 * RHS, LEAF), F32),
-            pltpu.VMEM((2 * RHS, BOXES * LEAF), F32),
             pltpu.SemaphoreType.DMA((6,)),
             pltpu.SemaphoreType.DMA((copies,)),
             pltpu.SemaphoreType.DMA((copies,)),
-            pltpu.SemaphoreType.DMA((PAIRS,)),
         ],
         compiler_params=pltpu.CompilerParams(
             collective_id=0, has_side_effects=True, vmem_limit_bytes=56 * 1024 * 1024
         ),
         name="adjoint",
-    )(near_list, signal, row_basis, transfer, column_basis, near_blocks)
+    )(near_list.T, signal, row_basis, transfer, column_basis, near_blocks)
 
 
 def solution(mesh):

time: 61.5 us -> 45.3 us (0.74)
  the two profiles are of different devices: /device:TPU:1 before, /device:TPU:8 now
where the time goes in v2:
time: 45.3 us; the launch traced here: 45.1 us
  Pallas kernels  43.4 us (96%)
  local copies, waits for them, and re-layouts  1.67 us (4%)
    pallas_call x1, Pallas kernels, shards(): pl.pallas_call(kernel, out_shape=jax.ShapeDtypeStruct((2 * RHS, BOXES * L...  43.4 us
    unnamed x1, local copies, waits for them, and re-layouts  1.67 us

profile of v2, /device:TPU:8, one launch (start us, length us, event | category | flops | bytes accessed | tf_op | source)
XLA Modules:
  0.0 45.1 jit_solution(2079867943011777844)
XLA Ops:
  0.0 43.4 %adjoint.1 = f32[32,2048]{1,0:T(8,128)} custom-call(s32[2,24]{1,0:T(2,128)} %bitcast.1, bf16[32,2048]{1,0:T(8,128)(2,1)} %sig_hbm.1, bf16[64,2048]{1,0:T(8,128)(2,1)} %row_hbm.1, bf16[16,13,32,128]{3,2,1,0:T(8,128)(2,1)} %tr_hbm.1, bf16[64,2048]{1,0:T(8,128)(2,1)} %col_hbm.1, bf16[24,128,256]{2,1,0:T(8,128)(2,1)} %near_hbm.1), custom_call_target="tpu_custom_call" | custom-call | tf_op jit(solution)/shard_map/adjoint/pallas_call | solution.py:411
  43.5 1.7 %copy.8 = f32[32,2048]{1,0:T(8,128)} copy(f32[32,2048]{1,0:T(8,128)} %adjoint.1) | data formatting | bytes 524288

commit v3 on v2

v3 whole, which is shorter than its diff:
```python
import functools

import jax
import jax.numpy as jnp
from jax import lax
from jax.experimental import pallas as pl
from jax.experimental.pallas import tpu as pltpu
from jax.sharding import PartitionSpec as P

LEAF = 128
BOXES = 16
PAIRS = 8
RHS = 16
CAP = 24
REACH = 4
LEVELS = 13
LOCAL = 4
GROUPS = 1
WIDTH = PAIRS // GROUPS
PHASES = (
    ((("sub", 0), ("sub", 1)), "receive"),
    ((("leaf", 0), ("leaf", 1)), "send"),
    ((("leaf", 2), ("leaf", 3)), "send"),
    ((("leaf", 4),), "one"),
    ((("leaf", 5), ("leaf", 6)), "send"),
)
FULL = 32767.0
SMALLEST = 1e-30

BF = jnp.bfloat16
F32 = jnp.float32
MESH = pl.DeviceIdType.MESH


def bit_of(index, bit):
    return (index // (1 << bit)) % 2


def flipped(index, bit):
    return index + (1 - 2 * bit_of(index, bit)) * (1 << bit)


def pieces(values):
    high = values.astype(BF)
    low = (values - high.astype(F32)).astype(BF)
    return jnp.concatenate([high, low], axis=0)


def folded(product):
    half = product.shape[0] // 2
    return product[:half] + product[half:]


def dot(left, right):
    return jnp.dot(left, right, preferred_element_type=F32)


def coded(coeffs):
    peak = jnp.abs(coeffs[0])
    for values in coeffs[1:]:
        peak = jnp.maximum(peak, jnp.abs(values))
    peak = jnp.maximum(jnp.maximum(peak[:8], peak[8:]), SMALLEST)
    inverse = FULL / peak
    inverse = jnp.concatenate([inverse, inverse], axis=0)
    codes = [jnp.round(values * inverse).astype(jnp.int32).astype(jnp.int16) for values in coeffs]
    return codes, peak * (1.0 / FULL)


def phase_plan():
    plan = []
    level = LOCAL
    slot = 0
    for bits, mode in PHASES:
        if mode == "one":
            plan.append((bits, level, mode, (bits,), None))
        else:
            low, high = bits
            plan.append((bits, level, mode, ((high,), (low, high), (low,)), slot))
            slot += 1
        level += len(bits)
    return tuple(plan), slot


PLAN, MERGED = phase_plan()
PARTNERS = sum(len(entry[3]) for entry in PLAN)
WEIGHTS = PARTNERS * GROUPS
HALO = WEIGHTS + MERGED
RIM = HALO + 2
COPIES = RIM + 2
CODE_ROWS = WIDTH * RHS
SCALE_ROWS = 16
SENT_ROWS = (
    PARTNERS * GROUPS * (CODE_ROWS + SCALE_ROWS)
    + MERGED * PAIRS * 32
    + 2 * 2 * REACH * 2 * RHS
    + 2 * REACH * 2 * RHS * 2
)


def kernel(
    list_hbm, sig_hbm, row_hbm, tr_hbm, col_hbm, near_hbm, out,
    sig, row, tr, col, near, window, mats, packed, far_tr, far_mats, basis, send_buf, recv_buf, send_scale, recv_scale,
    products, field, rim, list_ref, tally, load_sem, push_sem, pull_sem,
):
    leaf = lax.axis_index("leaf")
    sub = lax.axis_index("sub")
    leaves = lax.axis_size("leaf")
    subs = lax.axis_size("sub")

    loads = [
        pltpu.make_async_copy(sig_hbm, sig, load_sem.at[0]),
        pltpu.make_async_copy(row_hbm, row, load_sem.at[1]),
        pltpu.make_async_copy(tr_hbm.at[:, : LOCAL + 1], tr.at[:, : LOCAL + 1], load_sem.at[2]),
        pltpu.make_async_copy(tr_hbm.at[:, LOCAL + 1 :], tr.at[:, LOCAL + 1 :], load_sem.at[3]),
        pltpu.make_async_copy(near_hbm, near, load_sem.at[4]),
        pltpu.make_async_copy(col_hbm, col, load_sem.at[5]),
        pltpu.make_async_copy(list_hbm, list_ref, load_sem.at[6]),
    ]
    for load in loads:
        load.start()

    def partner(bits):
        places = {"leaf": leaf, "sub": sub}
        for axis, bit in bits:
            places[axis] = flipped(places[axis], bit)
        return places["leaf"], places["sub"]

    def side(step, which):
        axis, bit = PLAN[step][0][which]
        return bit_of(leaf if axis == "leaf" else sub, bit)

    rank = leaf * subs + sub
    after = (rank + 1) % (leaves * subs)
    before = (rank + leaves * subs - 1) % (leaves * subs)
    after = (after // subs, after % subs)
    before = (before // subs, before % subs)

    peers = [partner(bits) for entry in PLAN for bits in entry[3]]
    peers += [after, before]
    barrier = pltpu.get_barrier_semaphore()
    for peer in peers:
        pl.semaphore_signal(barrier, inc=1, device_id=peer, device_id_type=MESH)

    lane = lax.broadcasted_iota(jnp.int32, (32, LEAF), 1)
    group = lane // 32
    odd = (group % 2).astype(F32)
    upper = (group // 2).astype(F32)
    odd_b = odd.astype(BF)
    even_b = (1.0 - odd).astype(BF)
    sign_b = (1.0 - 2.0 * odd).astype(BF)
    upper_b = upper.astype(BF)
    lower_b = (1.0 - upper).astype(BF)
    first_half = lax.broadcasted_iota(jnp.int32, (RHS, LEAF), 1) < 64

    def turned(weights):
        by32, by64, by96 = (pltpu.roll(weights, shift, 1) for shift in (32, 64, 96))
        return (
            weights * sign_b,
            by96 * even_b + by32 * odd_b,
            by64 * sign_b,
            by32 * even_b + by96 * odd_b,
        )

    def expand(source, target, pairs=(0, PAIRS)):
        def body(pair, carry):
            s0, c0, sr0, cr0 = turned(source(2 * pair))
            s1, c1, sr1, cr1 = turned(source(2 * pair + 1))
            target[pair, 0] = jnp.concatenate(
                [s0 * lower_b, c0 * lower_b, sr1 * upper_b, cr1 * upper_b], axis=0
            )
            target[pair, 1] = jnp.concatenate(
                [sr0 * lower_b, cr0 * lower_b, s1 * upper_b, c1 * upper_b], axis=0
            )
            return carry

        lax.fori_loop(*pairs, body, 0, unroll=8)

    def expand_first(source, target):
        def body(pair, carry):
            s0, c0, sr0, cr0 = turned(source(2 * pair))
            s1, c1, sr1, cr1 = turned(source(2 * pair + 1))
            target[pair, 0] = jnp.concatenate(
                [
                    s0 * lower_b + sr1 * upper_b,
                    c0 * lower_b + cr1 * upper_b,
                    sr0 * lower_b + s1 * upper_b,
                    cr0 * lower_b + c1 * upper_b,
                ],
                axis=0,
            )
            return carry

        lax.fori_loop(0, PAIRS, body, 0, unroll=8)

    def expand_level(level):
        expand(lambda box: tr[box, level], mats.at[level])

    for load in loads[:3]:
        load.wait()
    def remote(source, target, number, peer):
        return pltpu.make_async_remote_copy(
            src_ref=source, dst_ref=target, send_sem=push_sem,
            recv_sem=pull_sem.at[number], device_id=peer, device_id_type=MESH,
        )

    weight_copies = {}
    for step, (_, _, mode, sets, slot) in enumerate(PLAN):
        if slot is not None:
            weight_copies[slot] = remote(
                packed.at[slot], far_tr.at[slot], WEIGHTS + slot,
                partner(sets[0] if mode == "receive" else sets[2]),
            )

    def pack(step):
        _, level, _, _, slot = PLAN[step]
        upper_child = (1 - side(step, 0)).astype(F32)
        straight = ((1.0 - upper) * (1.0 - upper_child)).astype(BF)
        straight_next = (upper * upper_child).astype(BF)
        turned_round = ((1.0 - upper) * upper_child).astype(BF)
        turned_next = (upper * (1.0 - upper_child)).astype(BF)
        for pair in range(PAIRS):
            one, two = tr[2 * pair, level], tr[2 * pair + 1, level]
            packed[slot, pair] = (
                one * straight
                + pltpu.roll(one, 64, 1) * turned_round
                + two * straight_next
                + pltpu.roll(two, 64, 1) * turned_next
            )

    pack(0)
    coeffs = []
    for pair in range(PAIRS):
        left, right = [], []
        for box in (2 * pair, 2 * pair + 1):
            points = slice(box * LEAF, (box + 1) * LEAF)
            samples = sig[:, points]
            window[2 * REACH + box] = samples
            left.append(jnp.concatenate([samples[:RHS], samples[RHS:]], axis=1))
            real, imag = row[:32, points], row[32:, points]
            right.append(
                jnp.concatenate(
                    [jnp.concatenate([real, imag], axis=1), jnp.concatenate([-imag, real], axis=1)],
                    axis=0,
                )
            )
        product = lax.dot_general(
            jnp.concatenate(left, axis=0), jnp.concatenate(right, axis=0),
            (((1,), (1,)), ((), ())), preferred_element_type=F32,
        )
        coeffs.append(jnp.where(first_half, product[:RHS], product[RHS:]))

    expand_first(lambda box: tr[box, 0], mats.at[0])
    for level in range(1, LOCAL):
        expand_level(level)

    pl.semaphore_wait(barrier, len(peers))
    weight_copies[0].start()

    coeffs = [folded(dot(pieces(coeffs[pair]), mats[0, pair, 0])) for pair in range(PAIRS)]
    for level in range(1, LOCAL):
        span = 1 << (level - 1)
        split = [pieces(values) for values in coeffs]
        following = []
        for pair in range(PAIRS):
            low = pair & ~span
            joined = jnp.concatenate([split[low], split[low | span]], axis=1)
            weights = mats[level, pair].reshape(2 * LEAF, LEAF)
            following.append(folded(dot(joined, weights)))
        coeffs = following

    edge = 2 * REACH
    halo = (
        remote(window.at[BOXES : BOXES + edge], window.at[:edge], HALO, after),
        remote(window.at[edge : 2 * edge], window.at[edge + BOXES :], HALO + 1, before),
    )

    def send_halo():
        for copy in halo:
            copy.start()

    def near_field():
        for copy in halo:
            copy.wait_recv()
        loads[4].wait()
        loads[6].wait()

        def multiply(slot, carry):
            picked = window[jnp.maximum(list_ref[0, slot], 0)]
            product = dot(picked, near[slot])
            real = product[:RHS, :LEAF] + product[RHS:, LEAF:]
            imag = product[RHS:, :LEAF] - product[:RHS, LEAF:]
            products[slot] = jnp.concatenate([real, imag], axis=0)
            return carry

        lax.fori_loop(0, CAP, multiply, 0, unroll=8)

        def gather(box, carry):
            total = jnp.zeros((2 * RHS, LEAF), F32)
            for slot in range(CAP):
                here = jnp.where(list_ref[1, slot] == box, 1.0, 0.0).astype(F32)
                total += products[slot] * here
            field[box] = total
            return carry

        lax.fori_loop(0, BOXES + 2 * REACH, gather, 0)

    rims = (
        remote(field.at[:REACH], rim.at[0], RIM, before),
        remote(field.at[BOXES + REACH :], rim.at[1], RIM + 1, after),
    )

    def send_rims():
        for copy in rims:
            copy.start()

    def expand_basis():
        loads[5].wait()
        for box in range(BOXES):
            points = slice(box * LEAF, (box + 1) * LEAF)
            real, imag = col[:32, points], col[32:, points]
            basis[box // 2, 64 * (box % 2) : 64 * (box % 2) + 64] = jnp.concatenate(
                [jnp.concatenate([real, imag], axis=1), jnp.concatenate([-imag, real], axis=1)],
                axis=0,
            )

    def finish_near():
        for copy in rims:
            copy.wait_recv()
        for place in range(REACH):
            field[REACH + place] += rim[1, place]
            field[BOXES + place] += rim[0, place]

    def finish(pair, values):
        zero = jnp.zeros_like(values)
        left = jnp.concatenate(
            [pieces(jnp.where(first_half, values, zero)), pieces(jnp.where(first_half, zero, values))],
            axis=0,
        )
        product = dot(left, basis[pair])
        for half in range(2):
            far_box = folded(product[2 * RHS * half : 2 * RHS * (half + 1)])
            box = 2 * pair + half
            points = slice(box * LEAF, (box + 1) * LEAF)
            near_box = field[REACH + box]
            out[:RHS, points] = far_box[:, :LEAF] + near_box[:RHS]
            out[RHS:, points] = far_box[:, LEAF:] + near_box[RHS:]

    def expand_far(slot):
        weight_copies[slot].wait_recv()
        for pair in range(PAIRS):
            weights = far_tr[slot, pair]
            signed = weights * sign_b
            crossed = pltpu.roll(weights, 96, 1) * even_b + pltpu.roll(weights, 32, 1) * odd_b
            far_mats[slot, pair] = jnp.concatenate(
                [signed * lower_b, crossed * lower_b, signed * upper_b, crossed * upper_b], axis=0
            )

    def fill(step):
        if step == 0:
            loads[3].wait()
            for later in range(1, len(PLAN)):
                if PLAN[later][4] is not None:
                    pack(later)
                    weight_copies[PLAN[later][4]].start()
            for level in range(LOCAL + 1, LEVELS):
                expand_level(level)
            expand_basis()
            expand_far(1)
            expand_far(0)
        elif step == 1:
            send_halo()
            expand_far(2)
        elif step == 2:
            expand_far(3)
            near_field()
            send_rims()

    first_number = []
    total = 0
    for entry in PLAN:
        first_number.append(total)
        total += len(entry[3])

    def number_of(step, group, order):
        return GROUPS * (first_number[step] + order) + group

    def push(step, group, which, values, orders):
        codes, scale = coded(values)
        for index, code in enumerate(codes):
            send_buf[2 * step + which, group, RHS * index : RHS * (index + 1)] = code
        send_scale[2 * step + which, group] = scale
        for order in orders:
            number = number_of(step, group, order)
            peer = partner(PLAN[step][3][order])
            remote(
                send_scale.at[2 * step + which, group], recv_scale.at[number], number, peer
            ).start()
            remote(send_buf.at[2 * step + which, group], recv_buf.at[number], number, peer).start()

    def arrived(step, group, order):
        number = number_of(step, group, order)
        both = tally.at[: CODE_ROWS + SCALE_ROWS]
        pltpu.make_async_copy(both, both, pull_sem.at[number]).wait()
        scale = recv_scale[number]
        scale = jnp.concatenate([scale, scale], axis=0)
        return [
            recv_buf[number, RHS * index : RHS * (index + 1)].astype(F32) * scale
            for index in range(WIDTH)
        ]

    def times(values, weights):
        return [folded(dot(pieces(values[index]), weights(index))) for index in range(WIDTH)]

    def sums(left, right):
        return [one + two for one, two in zip(left, right)]

    def matrices(level, group, child):
        return lambda index: mats[level, WIDTH * group + index, child]

    def send(step, group, values):
        _, level, mode, _, slot = PLAN[step]
        mine = matrices(level, group, side(step, 0))
        if mode == "one":
            push(step, group, 0, values, (0,))
            return lambda: times(values, mine)
        if mode == "receive":
            push(step, group, 0, values, (1, 2))
            if step == 0:
                expand_level(level)
            own = times(values, mine)
            push(step, group, 1, own, (0,))
            return lambda: own
        both = [
            folded(
                dot(
                    pieces(values[index]),
                    jnp.concatenate(
                        [mine(index), far_mats[slot, WIDTH * group + index]], axis=1
                    ),
                )
            )
            for index in range(WIDTH)
        ]
        own = [value[:, :LEAF] for value in both]
        push(step, group, 1, own, (0,))
        push(step, group, 0, [value[:, LEAF:] for value in both], (1, 2))
        return lambda: own

    coeffs = [coeffs[WIDTH * group : WIDTH * (group + 1)] for group in range(GROUPS)]
    partial = [send(0, group, coeffs[group])() for group in range(GROUPS)]
    for step, (bits, level, mode, sets, slot) in enumerate(PLAN):
        fill(step)
        for group in range(GROUPS):
            other = matrices(level, group, 1 - side(step, 0))
            if mode == "one":
                values = sums(partial[group], times(arrived(step, group, 0), other))
            else:
                values = arrived(step, group, 2)
                if mode == "receive":
                    values = times(values, other)
                values = sums(partial[group], values)
                mine_next = side(step, 1)
                ahead = times(values, matrices(level + 1, group, mine_next))
                far = arrived(step, group, 1)
                if mode == "receive":
                    far = times(far, lambda index: far_mats[slot, WIDTH * group + index])
                far = sums(far, arrived(step, group, 0))
                values = sums(ahead, times(far, matrices(level + 1, group, 1 - mine_next)))
            coeffs[group] = values
            if step + 1 < len(PLAN):
                partial[group] = send(step + 1, group, values)()
            else:
                if group == 0:
                    finish_near()
                for index in range(WIDTH):
                    finish(WIDTH * group + index, values[index])

    pltpu.make_async_copy(tally, tally, push_sem).wait()


def shards(signal, row_basis, transfer, column_basis, near_blocks, near_list):
    anywhere = pl.BlockSpec(memory_space=pltpu.HBM)
    return pl.pallas_call(
        kernel,
        out_shape=pltpu.VMEM((2 * RHS, BOXES * LEAF), F32),
        in_specs=[anywhere] * 6,
        out_specs=pl.BlockSpec(memory_space=pltpu.VMEM),
        scratch_shapes=[
            pltpu.VMEM((2 * RHS, BOXES * LEAF), BF),
            pltpu.VMEM((64, BOXES * LEAF), BF),
            pltpu.VMEM((BOXES, LEVELS, 32, LEAF), BF),
            pltpu.VMEM((64, BOXES * LEAF), BF),
            pltpu.VMEM((CAP, LEAF, 2 * LEAF), BF),
            pltpu.VMEM((BOXES + 4 * REACH, 2 * RHS, LEAF), BF),
            pltpu.VMEM((LEVELS, PAIRS, 2, LEAF, LEAF), BF),
            pltpu.VMEM((MERGED, PAIRS, 32, LEAF), BF),
            pltpu.VMEM((MERGED, PAIRS, 32, LEAF), BF),
            pltpu.VMEM((MERGED, PAIRS, LEAF, LEAF), BF),
            pltpu.VMEM((PAIRS, LEAF, 2 * LEAF), BF),
            pltpu.VMEM((2 * len(PLAN), GROUPS, CODE_ROWS, LEAF), jnp.int16),
            pltpu.VMEM((PARTNERS * GROUPS, CODE_ROWS, LEAF), jnp.int16),
            pltpu.VMEM((2 * len(PLAN), GROUPS, 8, LEAF), F32),
            pltpu.VMEM((PARTNERS * GROUPS, 8, LEAF), F32),
            pltpu.VMEM((CAP, 2 * RHS, LEAF), F32),
            pltpu.VMEM((BOXES + 2 * REACH, 2 * RHS, LEAF), F32),
            pltpu.VMEM((2, REACH, 2 * RHS, LEAF), F32),
            pltpu.SMEM((2, CAP), jnp.int32),
            pltpu.VMEM((SENT_ROWS, LEAF), BF),
            pltpu.SemaphoreType.DMA((7,)),
            pltpu.SemaphoreType.DMA,
            pltpu.SemaphoreType.DMA((COPIES,)),
        ],
        compiler_params=pltpu.CompilerParams(
            collective_id=0, has_side_effects=True, vmem_limit_bytes=56 * 1024 * 1024
        ),
        name="adjoint",
    )(near_list.T, signal, row_basis, transfer, column_basis, near_blocks)


def solution(mesh):
    return jax.shard_map(
        shards,
        mesh=mesh,
        in_specs=(
            P(None, ("leaf", "sub")),
            P(None, ("leaf", "sub")),
            P(("leaf", "sub"), None, None, None),
            P(None, ("leaf", "sub")),
            P(("leaf", "sub"), None, None),
            P(("leaf", "sub"), None),
        ),
        out_specs=P(None, ("leaf", "sub")),
        check_vma=False,
    )
```

time: 45.3 us -> 39.5 us (0.87)
  Pallas kernels: 43.4 us -> 38.6 us
  local copies, waits for them, and re-layouts: 1.67 us -> 0.71 us
    pallas_call x1, Pallas kernels: 43.4 us -> 38.6 us  [shards(): pl.pallas_call(kernel, out_shape=pltpu.VMEM((2 * RHS, BOXES * LEAF), F32)...]
    unnamed x1, local copies, waits for them, and re-layouts: 1.67 us -> 0.71 us
where the time goes in v3:
time: 39.5 us; the launch traced here: 39.4 us
  Pallas kernels  38.6 us (98%)
  local copies, waits for them, and re-layouts  0.71 us (2%)
    pallas_call x1, Pallas kernels, shards(): pl.pallas_call(kernel, out_shape=pltpu.VMEM((2 * RHS, BOXES * LEAF), F32)...  38.6 us

profile of v3, /device:TPU:8, one launch (start us, length us, event | category | flops | bytes accessed | tf_op | source)
XLA Modules:
  0.0 39.4 jit_solution(870944335038424361)
XLA Ops:
  0.0 38.6 %adjoint.1 = f32[32,2048]{1,0:T(8,128)S(1)} custom-call(s32[2,24]{1,0:T(2,128)} %bitcast.1, bf16[32,2048]{1,0:T(8,128)(2,1)} %sig_hbm.1, bf16[64,2048]{1,0:T(8,128)(2,1)} %row_hbm.1, bf16[16,13,32,128]{3,2,1,0:T(8,128)(2,1)} %tr_hbm.1, bf16[64,2048]{1,0:T(8,128)(2,1)} %col_hbm.1, bf16[24,128,256]{2,1,0:T(8,128)(2,1)} %near_hbm.1), custom_call_target="tpu_custom_call" | custom-call | tf_op jit(solution)/shard_map/adjoint/pallas_call | solution.py:483
  38.6 0.7 %copy.8 = f32[32,2048]{1,0:T(8,128)} copy(f32[32,2048]{1,0:T(8,128)S(1)} %adjoint.1) | data formatting | bytes 524288

commit v4 on v3

--- a/solution.py
+++ b/solution.py
@@ -15,7 +15,7 @@
 REACH = 4
 LEVELS = 13
 LOCAL = 4
-GROUPS = 1
+GROUPS = 2
 WIDTH = PAIRS // GROUPS
 PHASES = (
     ((("sub", 0), ("sub", 1)), "receive"),
@@ -26,6 +26,7 @@
 )
 FULL = 32767.0
 SMALLEST = 1e-30
+STEPS = 64.0
 
 BF = jnp.bfloat16
 F32 = jnp.float32
@@ -60,10 +61,12 @@
     for values in coeffs[1:]:
         peak = jnp.maximum(peak, jnp.abs(values))
     peak = jnp.maximum(jnp.maximum(peak[:8], peak[8:]), SMALLEST)
-    inverse = FULL / peak
+    power = jnp.ceil(jnp.log2(peak * (1.0 / FULL)) * STEPS + 0.125)
+    inverse = jnp.exp2(power * (-1.0 / STEPS))
     inverse = jnp.concatenate([inverse, inverse], axis=0)
-    codes = [jnp.round(values * inverse).astype(jnp.int32).astype(jnp.int16) for values in coeffs]
-    return codes, peak * (1.0 / FULL)
+    codes = [jnp.round(values * inverse) for values in coeffs]
+    codes.append(power)
+    return [code.astype(jnp.int32).astype(jnp.int16) for code in codes]
 
 
 def phase_plan():
@@ -87,10 +90,9 @@
 HALO = WEIGHTS + MERGED
 RIM = HALO + 2
 COPIES = RIM + 2
-CODE_ROWS = WIDTH * RHS
-SCALE_ROWS = 16
+CODE_ROWS = WIDTH * RHS + 8
 SENT_ROWS = (
-    PARTNERS * GROUPS * (CODE_ROWS + SCALE_ROWS)
+    PARTNERS * GROUPS * CODE_ROWS
     + MERGED * PAIRS * 32
     + 2 * 2 * REACH * 2 * RHS
     + 2 * REACH * 2 * RHS * 2
@@ -99,7 +101,7 @@
 
 def kernel(
     list_hbm, sig_hbm, row_hbm, tr_hbm, col_hbm, near_hbm, out,
-    sig, row, tr, col, near, window, mats, packed, far_tr, far_mats, basis, send_buf, recv_buf, send_scale, recv_scale,
+    sig, row, tr, col, near, window, mats, packed, far_tr, far_mats, basis, send_buf, recv_buf,
     products, field, rim, list_ref, tally, load_sem, push_sem, pull_sem,
 ):
     leaf = lax.axis_index("leaf")
@@ -250,7 +252,7 @@
         coeffs.append(jnp.where(first_half, product[:RHS], product[RHS:]))
 
     expand_first(lambda box: tr[box, 0], mats.at[0])
-    for level in range(1, LOCAL):
+    for level in range(1, LOCAL + 1):
         expand_level(level)
 
     pl.semaphore_wait(barrier, len(peers))
@@ -384,29 +386,31 @@
     def number_of(step, group, order):
         return GROUPS * (first_number[step] + order) + group
 
+    def message(step, group, which, order):
+        number = number_of(step, group, order)
+        return remote(
+            send_buf.at[2 * step + which, group], recv_buf.at[number], number,
+            partner(PLAN[step][3][order]),
+        )
+
     def push(step, group, which, values, orders):
-        codes, scale = coded(values)
+        *codes, power = coded(values)
         for index, code in enumerate(codes):
             send_buf[2 * step + which, group, RHS * index : RHS * (index + 1)] = code
-        send_scale[2 * step + which, group] = scale
+        send_buf[2 * step + which, group, WIDTH * RHS :] = power
         for order in orders:
-            number = number_of(step, group, order)
-            peer = partner(PLAN[step][3][order])
-            remote(
-                send_scale.at[2 * step + which, group], recv_scale.at[number], number, peer
-            ).start()
-            remote(send_buf.at[2 * step + which, group], recv_buf.at[number], number, peer).start()
+            message(step, group, which, order).start()
 
     def arrived(step, group, order):
         number = number_of(step, group, order)
-        both = tally.at[: CODE_ROWS + SCALE_ROWS]
-        pltpu.make_async_copy(both, both, pull_sem.at[number]).wait()
-        scale = recv_scale[number]
-        scale = jnp.concatenate([scale, scale], axis=0)
-        return [
-            recv_buf[number, RHS * index : RHS * (index + 1)].astype(F32) * scale
+        message(step, group, 0, order).wait_recv()
+        tiles = [
+            recv_buf[number, RHS * index : RHS * (index + 1)].astype(F32)
             for index in range(WIDTH)
         ]
+        scale = jnp.exp2(recv_buf[number, WIDTH * RHS :].astype(F32) * (1.0 / STEPS))
+        scale = jnp.concatenate([scale, scale], axis=0)
+        return [tile * scale for tile in tiles]
 
     def times(values, weights):
         return [folded(dot(pieces(values[index]), weights(index))) for index in range(WIDTH)]
@@ -425,8 +429,6 @@
             return lambda: times(values, mine)
         if mode == "receive":
             push(step, group, 0, values, (1, 2))
-            if step == 0:
-                expand_level(level)
             own = times(values, mine)
             push(step, group, 1, own, (0,))
             return lambda: own
@@ -460,12 +462,26 @@
                     values = times(values, other)
                 values = sums(partial[group], values)
                 mine_next = side(step, 1)
-                ahead = times(values, matrices(level + 1, group, mine_next))
+                first = matrices(level + 1, group, mine_next)
+                second = matrices(level + 1, group, 1 - mine_next)
+                if group == 0:
+                    ahead = times(values, first)
                 far = arrived(step, group, 1)
                 if mode == "receive":
                     far = times(far, lambda index: far_mats[slot, WIDTH * group + index])
                 far = sums(far, arrived(step, group, 0))
-                values = sums(ahead, times(far, matrices(level + 1, group, 1 - mine_next)))
+                if group == 0:
+                    values = sums(ahead, times(far, second))
+                else:
+                    values = [
+                        folded(
+                            dot(
+                                jnp.concatenate([pieces(values[index]), pieces(far[index])], axis=1),
+                                jnp.concatenate([first(index), second(index)], axis=0),
+                            )
+                        )
+                        for index in range(WIDTH)
+                    ]
             coeffs[group] = values
             if step + 1 < len(PLAN):
                 partial[group] = send(step + 1, group, values)()
@@ -499,8 +515,6 @@
             pltpu.VMEM((PAIRS, LEAF, 2 * LEAF), BF),
             pltpu.VMEM((2 * len(PLAN), GROUPS, CODE_ROWS, LEAF), jnp.int16),
             pltpu.VMEM((PARTNERS * GROUPS, CODE_ROWS, LEAF), jnp.int16),
-            pltpu.VMEM((2 * len(PLAN), GROUPS, 8, LEAF), F32),
-            pltpu.VMEM((PARTNERS * GROUPS, 8, LEAF), F32),
             pltpu.VMEM((CAP, 2 * RHS, LEAF), F32),
             pltpu.VMEM((BOXES + 2 * REACH, 2 * RHS, LEAF), F32),
             pltpu.VMEM((2, REACH, 2 * RHS, LEAF), F32),

time: 39.5 us -> 38.3 us (0.970)
  Pallas kernels: 38.6 us -> 37.5 us
    pallas_call x1, Pallas kernels: 38.6 us -> 37.5 us  [shards(): pl.pallas_call(kernel, out_shape=pltpu.VMEM((2 * RHS, BOXES * LEAF), F32)...]
where the time goes in v4:
time: 38.3 us; the launch traced here: 38.2 us
  Pallas kernels  37.5 us (98%)
  local copies, waits for them, and re-layouts  0.71 us (2%)
    pallas_call x1, Pallas kernels, shards(): pl.pallas_call(kernel, out_shape=pltpu.VMEM((2 * RHS, BOXES * LEAF), F32)...  37.5 us

profile of v4, /device:TPU:8, one launch (start us, length us, event | category | flops | bytes accessed | tf_op | source)
XLA Modules:
  0.0 38.2 jit_solution(8641229767757524775)
XLA Ops:
  0.0 37.5 %adjoint.1 = f32[32,2048]{1,0:T(8,128)S(1)} custom-call(s32[2,24]{1,0:T(2,128)} %bitcast.1, bf16[32,2048]{1,0:T(8,128)(2,1)} %sig_hbm.1, bf16[64,2048]{1,0:T(8,128)(2,1)} %row_hbm.1, bf16[16,13,32,128]{3,2,1,0:T(8,128)(2,1)} %tr_hbm.1, bf16[64,2048]{1,0:T(8,128)(2,1)} %col_hbm.1, bf16[24,128,256]{2,1,0:T(8,128)(2,1)} %near_hbm.1), custom_call_target="tpu_custom_call" | custom-call | tf_op jit(solution)/shard_map/adjoint/pallas_call | solution.py:499
  37.5 0.7 %copy.8 = f32[32,2048]{1,0:T(8,128)} copy(f32[32,2048]{1,0:T(8,128)S(1)} %adjoint.1) | data formatting | bytes 524288

commit v5 on v4

--- a/solution.py
+++ b/solution.py
@@ -87,7 +87,7 @@
 PLAN, MERGED = phase_plan()
 PARTNERS = sum(len(entry[3]) for entry in PLAN)
 WEIGHTS = PARTNERS * GROUPS
-HALO = WEIGHTS + MERGED
+HALO = WEIGHTS + MERGED * GROUPS
 RIM = HALO + 2
 COPIES = RIM + 2
 CODE_ROWS = WIDTH * RHS + 8
@@ -208,10 +208,13 @@
     weight_copies = {}
     for step, (_, _, mode, sets, slot) in enumerate(PLAN):
         if slot is not None:
-            weight_copies[slot] = remote(
-                packed.at[slot], far_tr.at[slot], WEIGHTS + slot,
-                partner(sets[0] if mode == "receive" else sets[2]),
-            )
+            for group in range(GROUPS):
+                pairs = pl.ds(WIDTH * group, WIDTH)
+                weight_copies[slot, group] = remote(
+                    packed.at[slot, pairs], far_tr.at[slot, pairs],
+                    WEIGHTS + GROUPS * slot + group,
+                    partner(sets[0] if mode == "receive" else sets[2]),
+                )
 
     def pack(step):
         _, level, _, _, slot = PLAN[step]
@@ -256,7 +259,8 @@
         expand_level(level)
 
     pl.semaphore_wait(barrier, len(peers))
-    weight_copies[0].start()
+    for group in range(GROUPS):
+        weight_copies[0, group].start()
 
     coeffs = [folded(dot(pieces(coeffs[pair]), mats[0, pair, 0])) for pair in range(PAIRS)]
     for level in range(1, LOCAL):
@@ -347,9 +351,10 @@
             out[:RHS, points] = far_box[:, :LEAF] + near_box[:RHS]
             out[RHS:, points] = far_box[:, LEAF:] + near_box[RHS:]
 
-    def expand_far(slot):
-        weight_copies[slot].wait_recv()
-        for pair in range(PAIRS):
+    def expand_far(slot, groups=range(GROUPS)):
+        for group in groups:
+            weight_copies[slot, group].wait_recv()
+        for pair in range(WIDTH * groups[0], WIDTH * (groups[-1] + 1)):
             weights = far_tr[slot, pair]
             signed = weights * sign_b
             crossed = pltpu.roll(weights, 96, 1) * even_b + pltpu.roll(weights, 32, 1) * odd_b
@@ -363,12 +368,12 @@
             for later in range(1, len(PLAN)):
                 if PLAN[later][4] is not None:
                     pack(later)
-                    weight_copies[PLAN[later][4]].start()
+                    for group in range(GROUPS):
+                        weight_copies[PLAN[later][4], group].start()
             for level in range(LOCAL + 1, LEVELS):
                 expand_level(level)
             expand_basis()
             expand_far(1)
-            expand_far(0)
         elif step == 1:
             send_halo()
             expand_far(2)
@@ -454,6 +459,8 @@
         fill(step)
         for group in range(GROUPS):
             other = matrices(level, group, 1 - side(step, 0))
+            if step == 0:
+                expand_far(0, (group,))
             if mode == "one":
                 values = sums(partial[group], times(arrived(step, group, 0), other))
             else:

time: 38.3 us -> 38.2 us (level)
  no operation moved by 1% of the time
where the time goes in v5:
time: 38.2 us; the launch traced here: 38.1 us
  Pallas kernels  37.4 us (98%)
  local copies, waits for them, and re-layouts  0.71 us (2%)
    pallas_call x1, Pallas kernels, shards(): pl.pallas_call(kernel, out_shape=pltpu.VMEM((2 * RHS, BOXES * LEAF), F32)...  37.4 us

profile of v5, /device:TPU:8, one launch (start us, length us, event | category | flops | bytes accessed | tf_op | source)
XLA Modules:
  0.0 38.1 jit_solution(4665399697472381272)
XLA Ops:
  0.0 37.4 %adjoint.1 = f32[32,2048]{1,0:T(8,128)S(1)} custom-call(s32[2,24]{1,0:T(2,128)} %bitcast.1, bf16[32,2048]{1,0:T(8,128)(2,1)} %sig_hbm.1, bf16[64,2048]{1,0:T(8,128)(2,1)} %row_hbm.1, bf16[16,13,32,128]{3,2,1,0:T(8,128)(2,1)} %tr_hbm.1, bf16[64,2048]{1,0:T(8,128)(2,1)} %col_hbm.1, bf16[24,128,256]{2,1,0:T(8,128)(2,1)} %near_hbm.1), custom_call_target="tpu_custom_call" | custom-call | tf_op jit(solution)/shard_map/adjoint/pallas_call | solution.py:506
  37.4 0.7 %copy.8 = f32[32,2048]{1,0:T(8,128)} copy(f32[32,2048]{1,0:T(8,128)S(1)} %adjoint.1) | data formatting | bytes 524288
